TPU v7x, 32 devices: a whole 2x2x4 slice. The times are simulated.
32 devices in a mesh: seq: 8 (over z, x), head: 4 (over y, core).
Axes of the slice: x: 2, y: 2, z: 4, core: 2. Of those that a mesh axis runs over, the one named last changes fastest.
Arguments:
- stream: bfloat16 [4096, 5120], P('seq', 'head'), may hold values from -6 to 6
- gate_input: bfloat16 [4096, 5120], P('seq', 'head'), may hold values from -6 to 6
- in_coeff: bfloat16 [4096, 128], P('seq'), may hold values from -0.5 to 0.5
- out_coeff: bfloat16 [4096, 128], P('seq'), may hold values from -0.5 to 0.5
- step_raw: float32 [80, 4096], P('head', 'seq'), may hold values from -4 to 4
- step_bias: float32 [80], P('head'), may hold values from -1 to 1
- decay_rate: float32 [80], P('head'), may hold values from 0.00024414062 to 0.05
- skip_scale: float32 [80], P('head'), may hold values from 0.5 to 5
- norm_gain: float32 [5120], P('head'), may hold values from 0.1 to 1.9
- out_proj: bfloat16 [5120, 2560], P('head'), may hold values from -0.078125 to 0.078125
- doc_starts: int32 [16], replicated, may hold values from 0 to 4095, as said below
Outputs:
- layer_out: bfloat16 [4096, 2560], P(('seq', 'head'))
Inputs may be any that keep to these rules, and one draw needn't show every extreme that they name: `doc_starts`: the first entry is 0, the last is 4095, and the entries strictly increase; entry i is the position where document i begins.
All inputs are finite; a program needn't handle non-finite values.
Results may differ from a plain program's by a relative error of at most 0.01.
Values may be sent and summed in bfloat16 or wider, within the bound.
A program may use at most 128 MiB of HBM per device.

v0:
```python
import functools

import jax
import jax.numpy as jnp
from jax import lax
from jax.experimental import pallas as pl
from jax.experimental.pallas import tpu as pltpu
from jax.sharding import PartitionSpec as P

EPSILON = 1e-05
F32 = jnp.float32
BF16 = jnp.bfloat16
MESH = pl.DeviceIdType.MESH
LAG = 2
SPLIT = 2
FAR_LAG = 2


def dot(a, b, ca, cb):
    return lax.dot_general(a, b, (((ca,), (cb,)), ((), ())), preferred_element_type=F32)


def split(value, parts):
    pieces = []
    for _ in range(parts):
        piece = value.astype(BF16).astype(F32)
        pieces.append(piece)
        value = value - piece
    return jnp.concatenate(pieces, axis=0).astype(BF16)


def to_column(row):
    n = row.shape[1]
    eye = lax.broadcasted_iota(jnp.int32, (n, n), 0) == lax.broadcasted_iota(jnp.int32, (n, n), 1)
    return jnp.sum(jnp.where(eye, row, 0.0), axis=1, keepdims=True)


def kernel(
    n_seq,
    n_head,
    heads,
    chunks,
    pieces,
    starts_hbm,
    step_hbm,
    bias_hbm,
    rate_hbm,
    skip_hbm,
    gain_hbm,
    in_hbm,
    out_hbm,
    stream_hbm,
    gate_hbm,
    proj_hbm,
    result_ref,
    starts_ref,
    step_ref,
    bias_ref,
    rate_ref,
    skip_ref,
    gain_ref,
    in_ref,
    out_ref,
    stream,
    gate,
    proj,
    pad,
    expand,
    factor_in,
    factor_out,
    pairs,
    carry_in,
    source,
    summary,
    link_own,
    link_prev,
    before_gate,
    base,
    slope,
    square,
    hidden,
    chain_out,
    chain_in,
    cross_in,
    square_out,
    square_in,
    held,
    near_out,
    near_in,
    far_out,
    far_in,
    small_sem,
    load_sem,
    link_sem,
    chain_sem,
    cross_sem,
    square_sem,
    near_sem,
    far_sem,
):
    rows, channels = stream.shape
    state = in_ref.shape[1]
    width = channels // chunks
    head_size = channels // heads
    padded = pad.shape[0]
    sub = width // SPLIT
    half = rows // 2
    share = rows // n_head
    piece = proj.shape[1] // pieces

    s = lax.axis_index("seq")
    g = lax.axis_index("head")
    parity = s % 2
    pair = s // 2
    last_pair = n_seq // 2 - 1
    core = g % 2
    side = g // 2
    near = side * 2 + (1 - core)
    far = (1 - side) * 2 + core
    cross = s + 1 - 2 * parity
    peers = (near, far, (1 - side) * 2 + (1 - core))

    loads = [
        pltpu.make_async_copy(src, dst, load_sem.at[i])
        for i, (src, dst) in enumerate(((stream_hbm, stream), (gate_hbm, gate), (proj_hbm, proj)))
    ]
    smalls = [
        pltpu.make_async_copy(src, dst, small_sem.at[i])
        for i, (src, dst) in enumerate(
            (
                (step_hbm, step_ref),
                (bias_hbm, bias_ref),
                (rate_hbm, rate_ref),
                (starts_hbm, starts_ref),
                (in_hbm, in_ref),
                (skip_hbm, skip_ref),
                (gain_hbm, gain_ref),
                (out_hbm, out_ref),
            )
        )
    ]
    for small in smalls[:3]:
        small.start()
    loads[0].start()
    for small in smalls[3:]:
        small.start()

    barrier = pltpu.get_barrier_semaphore()
    for step in (1, 2, n_seq - 2, n_seq - 1):
        pl.semaphore_signal(barrier, inc=1, device_id=((s + step) % n_seq, g), device_id_type=MESH)
    for peer in peers:
        pl.semaphore_signal(barrier, inc=1, device_id=(s, peer), device_id_type=MESH)

    def send(src, dst, sems, seq, head):
        return pltpu.make_async_remote_copy(
            src_ref=src,
            dst_ref=dst,
            send_sem=sems.at[0],
            recv_sem=sems.at[1],
            device_id=(seq, head),
            device_id_type=MESH,
        )

    link_copy = send(link_own, link_prev, link_sem, (s + 1) % n_seq, g)

    def chain_copy(k):
        return send(
            chain_out.at[k], chain_in.at[k], chain_sem.at[k], (s + 2) % n_seq, g
        )

    def cross_copy(k, even):
        source_ref = chain_out if even else chain_in
        return send(source_ref.at[k], cross_in.at[k], cross_sem.at[k], cross, g)

    pad[...] = jnp.zeros_like(pad)
    for small in smalls:
        small.wait()
    raw = step_ref[...] + to_column(bias_ref[...])
    pad[pl.ds(0, heads), :] = jnp.maximum(raw, 0.0) + jnp.log(1.0 + jnp.exp(-jnp.abs(raw)))
    step_size = pad[...]
    head_row = lax.broadcasted_iota(jnp.int32, (padded, channels), 0) * head_size
    lane = lax.broadcasted_iota(jnp.int32, (padded, channels), 1)
    spread = jnp.where((lane >= head_row) & (lane < head_row + head_size), 1.0, 0.0)
    expand[...] = jnp.concatenate([spread, spread], axis=0).astype(BF16)
    rate = to_column(rate_ref[...])
    if padded > heads:
        rate = jnp.concatenate([rate, jnp.zeros((padded - heads, 1), F32)], axis=0)
    log_decay = -step_size * rate
    first = lax.broadcasted_iota(jnp.int32, (rows, rows), 0)
    second = lax.broadcasted_iota(jnp.int32, (rows, rows), 1)
    upper = jnp.where(first <= second, 1.0, 0.0).astype(BF16)
    sums = dot(split(log_decay, 3), upper, 1, 0)
    cumulative = sums[:padded] + sums[padded : 2 * padded] + sums[2 * padded :]
    middle = cumulative[:, half - 1 : half]
    last = cumulative[:, rows - 1 : rows]
    factor_in[...] = split(jnp.exp(middle - cumulative) * step_size, 2)

    starts = starts_ref[...].astype(F32).reshape(1, -1)
    offset = s * rows
    place = (offset + lax.broadcasted_iota(jnp.int32, (rows, 1), 0)).astype(F32)
    place_lane = (offset + lax.broadcasted_iota(jnp.int32, (1, rows), 1)).astype(F32)
    doc = jnp.sum(jnp.where(starts <= place, 1.0, 0.0), axis=1, keepdims=True)
    before = jnp.sum(jnp.where(starts <= (offset - 1).astype(F32), 1.0, 0.0), axis=1, keepdims=True)
    doc_end = doc[rows - 1 : rows, :]
    joined_end = jnp.where(doc_end == before, 1.0, 0.0)

    def per_channel(column):
        return jnp.sum(spread * column, axis=0, keepdims=True)

    link_own[...] = per_channel(jnp.exp(last)) * joined_end
    end_gate = per_channel(jnp.exp(last - middle))
    before_gate[1:2, :] = end_gate
    in_end = jnp.where(doc == doc_end, in_ref[...].astype(F32), 0.0).astype(BF16)

    pl.semaphore_wait(barrier, 4 + len(peers))

    @pl.when(s < n_seq - 1)
    def _():
        link_copy.start()

    loads[0].wait()
    loads[1].start()
    loads[2].start()

    def columns(k):
        return pl.ds(pl.multiple_of(k * width, width), width)

    def make_summary(k, _):
        cols = columns(k)
        scale = dot(factor_in[...], expand[:, cols], 0, 0)
        scaled = (stream[:, cols].astype(F32) * scale).astype(BF16)
        source[:, cols] = scaled
        fresh = dot(in_end, scaled, 0, 0) * before_gate[1:2, cols]

        @pl.when(pair == 0)
        def _():
            for i in range(SPLIT):
                at = k * SPLIT + i
                chain_out[at] = fresh[:, i * sub : (i + 1) * sub].astype(BF16)
                chain_in[at] = jnp.zeros((state, sub), BF16)
                if last_pair > 0:
                    chain_copy(at).start()

                @pl.when(parity == 0)
                def _():
                    cross_in[at] = jnp.zeros((state, sub), BF16)
                    cross_copy(at, True).start()

        @pl.when(pair > 0)
        def _():
            for i in range(SPLIT):
                summary[k * SPLIT + i] = fresh[:, i * sub : (i + 1) * sub]

        return 0

    lax.fori_loop(0, chunks, make_summary, 0)

    factor_out[...] = split(jnp.exp(cumulative - middle), 2)
    before_gate[3:4, :] = gain_ref[...].reshape(1, -1)
    doc_lane = jnp.sum(jnp.where(to_column(starts) <= place_lane, 1.0, 0.0), axis=0, keepdims=True)
    before_gate[0:1, :] = per_channel(jnp.exp(middle))
    skip = to_column(skip_ref[...])
    if padded > heads:
        skip = jnp.concatenate([skip, jnp.zeros((padded - heads, 1), F32)], axis=0)
    before_gate[2:3, :] = per_channel(skip)
    carry_in[...] = jnp.where(doc == before, out_ref[...].astype(F32), 0.0).astype(BF16)
    scores = dot(out_ref[...], in_ref[...], 1, 1)
    live = (first >= second) & (doc == doc_lane)
    pairs[...] = jnp.where(live, scores, 0.0).astype(BF16)
    square[...] = jnp.zeros_like(square)
    loads[1].wait()

    @pl.when(s > 0)
    def _():
        link_copy.wait_recv()

    @pl.when(s == 0)
    def _():
        link_prev[...] = jnp.zeros_like(link_prev)

    def local_part(k):
        cols = columns(k)
        gate_value = gate[:, cols].astype(F32)
        silu = gate_value * (0.5 * jnp.tanh(0.5 * gate_value) + 0.5)
        within = jnp.concatenate(
            [
                dot(pairs[:half, :half], source[:half, cols], 1, 0),
                dot(pairs[half:, :], source[:, cols], 1, 0),
            ],
            axis=0,
        )
        factor = dot(factor_out[...], expand[:, cols], 0, 0) * silu
        slope[:, cols] = factor
        base[:, cols] = within * factor + stream[:, cols].astype(F32) * before_gate[2:3, cols] * silu

    def forward(k):
        @pl.when(pair > 0)
        def _():
            chain_copy(k).wait_recv()

            @pl.when(parity == 1)
            def _():
                cross_copy(k, False).start()

            cols = pl.ds(pl.multiple_of(k * sub, sub), sub)
            longer = link_own[:, cols] * link_prev[:, cols] * chain_in[k].astype(F32)
            chain_out[k] = (longer + summary[k]).astype(BF16)

            @pl.when(pair < last_pair)
            def _():
                chain_copy(k).start()

            @pl.when(parity == 0)
            def _():
                cross_copy(k, True).start()

    def finish(k):
        @pl.when(s > 0)
        def _():
            for i in range(SPLIT):
                cross_copy(k * SPLIT + i, True).wait_recv()

        cols = columns(k)
        own = jnp.concatenate([chain_in[k * SPLIT + i].astype(F32) for i in range(SPLIT)], axis=1)
        other = jnp.concatenate([cross_in[k * SPLIT + i].astype(F32) for i in range(SPLIT)], axis=1)
        incoming = link_prev[:, cols] * own + other
        incoming = (incoming * before_gate[0:1, cols]).astype(BF16)
        carried = dot(carry_in[...], incoming, 1, 0)
        gated = base[:, cols] + slope[:, cols] * carried
        hidden[:, cols] = (gated * before_gate[3:4, cols]).astype(BF16)
        squares = gated * gated
        total = square[...]
        for i in range(width // 128):
            total = total + squares[:, i * 128 : (i + 1) * 128]
        square[...] = total

    def main_step(k, _):
        @pl.when(k < chunks)
        def _():
            local_part(k)
            for i in range(SPLIT):
                forward(k * SPLIT + i)

        @pl.when(k >= LAG)
        def _():
            finish(k - LAG)

        return 0

    lax.fori_loop(0, chunks + LAG, main_step, 0)

    loads[2].wait()

    def piece_columns(j):
        return pl.ds(pl.multiple_of(j * piece, piece), piece)

    def near_copy(stage, j):
        at = stage * pieces + j
        return send(near_out.at[at], near_in.at[at], near_sem.at[at], s, near)

    def far_copy(j):
        return send(far_out.at[j], far_in.at[j], far_sem.at[j], s, far)

    def half_rows(which):
        return pl.ds(pl.multiple_of(which * 2 * share, 2 * share), 2 * share)

    def core_rows(which):
        return pl.ds(pl.multiple_of(which * share, share), share)

    def project(stage, which, j):
        held[stage * pieces + j] = dot(hidden[half_rows(which), :], proj[:, piece_columns(j)], 1, 0)
        near_out[stage * pieces + j] = held[stage * pieces + j, core_rows(1 - core), :].astype(BF16)
        near_copy(stage, j).start()

    def pass_on(j):
        near_copy(0, j).wait_recv()
        both = held[j, core_rows(core), :] + near_in[j].astype(F32)
        far_out[j] = both.astype(BF16)
        far_copy(j).start()

    def far_step(j, _):
        @pl.when(j < pieces)
        def _():
            project(0, 1 - side, j)

        @pl.when(j >= FAR_LAG)
        def _():
            pass_on(j - FAR_LAG)

        return 0

    lax.fori_loop(0, pieces + FAR_LAG, far_step, 0)

    for owner in range(n_head):
        block = square[owner * share : (owner + 1) * share, :]
        sums_lane = jnp.sum(block.T, axis=0, keepdims=True)
        square_out[owner] = jnp.broadcast_to(sums_lane, (8, share))
    for i, peer in enumerate(peers):
        send(square_out.at[peer], square_in.at[i], square_sem.at[i], s, peer).start()

    def near_step(j, _):
        project(1, side, j)
        return 0

    lax.fori_loop(0, pieces, near_step, 0)

    total = square_out[g]
    for i, peer in enumerate(peers):
        send(square_out.at[peer], square_in.at[i], square_sem.at[i], s, peer).wait()
        total = total + square_in[i]
    mean = jnp.broadcast_to(total[0:1, :], (128, share)).T / (channels * n_head)
    scale_row = lax.rsqrt(mean + EPSILON)[:, 0:1]

    def collect(j, _):
        near_copy(1, j).wait_recv()
        far_copy(j).wait_recv()
        at = pieces + j
        whole = held[at, core_rows(core), :] + near_in[at].astype(F32) + far_in[j].astype(F32)
        result_ref[:, piece_columns(j)] = (whole * scale_row).astype(BF16)
        return 0

    lax.fori_loop(0, pieces, collect, 0)

    @pl.when(s < n_seq - 1)
    def _():
        link_copy.wait_send()

    def drain(k, _):
        @pl.when(pair < last_pair)
        def _():
            chain_copy(k).wait_send()

        @pl.when(parity == 0)
        def _():
            cross_copy(k, True).wait_send()

        @pl.when((parity == 1) & (pair > 0))
        def _():
            cross_copy(k, False).wait_send()

        return 0

    lax.fori_loop(0, chunks * SPLIT, drain, 0)

    def drain_pieces(j, _):
        near_copy(0, j).wait_send()
        near_copy(1, j).wait_send()
        far_copy(j).wait_send()
        return 0

    lax.fori_loop(0, pieces, drain_pieces, 0)


def local(
    n_seq,
    n_head,
    stream,
    gate_input,
    in_coeff,
    out_coeff,
    step_raw,
    step_bias,
    decay_rate,
    skip_scale,
    norm_gain,
    out_proj,
    doc_starts,
):
    rows, channels = stream.shape
    heads = step_raw.shape[0]
    state = in_coeff.shape[1]
    model = out_proj.shape[1]
    chunks, pieces = channels // 256, model // 256
    width, piece = channels // chunks, model // pieces
    parts, sub = chunks * SPLIT, width // SPLIT
    padded = -(-heads // 8) * 8
    share = rows // n_head
    assert n_head == 4 and n_seq % 2 == 0 and rows <= 512
    vmem = pl.BlockSpec(memory_space=pltpu.VMEM)
    anywhere = pl.BlockSpec(memory_space=pl.ANY)
    dma = pltpu.SemaphoreType.DMA
    return pl.pallas_call(
        functools.partial(kernel, n_seq, n_head, heads, chunks, pieces),
        out_shape=jax.ShapeDtypeStruct((share, model), BF16),
        in_specs=[anywhere] * 11,
        out_specs=vmem,
        scratch_shapes=[
            pltpu.VMEM(doc_starts.shape, doc_starts.dtype),
            pltpu.VMEM(step_raw.shape, F32),
            pltpu.VMEM((1, heads), F32),
            pltpu.VMEM((1, heads), F32),
            pltpu.VMEM((1, heads), F32),
            pltpu.VMEM(norm_gain.shape, F32),
            pltpu.VMEM(in_coeff.shape, BF16),
            pltpu.VMEM(out_coeff.shape, BF16),
            pltpu.VMEM((rows, channels), BF16),
            pltpu.VMEM((rows, channels), BF16),
            pltpu.VMEM((channels, model), BF16),
            pltpu.VMEM((padded, rows), F32),
            pltpu.VMEM((2 * padded, channels), BF16),
            pltpu.VMEM((2 * padded, rows), BF16),
            pltpu.VMEM((2 * padded, rows), BF16),
            pltpu.VMEM((rows, rows), BF16),
            pltpu.VMEM((rows, state), BF16),
            pltpu.VMEM((rows, channels), BF16),
            pltpu.VMEM((parts, state, sub), F32),
            pltpu.VMEM((1, channels), F32),
            pltpu.VMEM((1, channels), F32),
            pltpu.VMEM((8, channels), F32),
            pltpu.VMEM((rows, channels), F32),
            pltpu.VMEM((rows, channels), F32),
            pltpu.VMEM((rows, 128), F32),
            pltpu.VMEM((rows, channels), BF16),
            pltpu.VMEM((parts, state, sub), BF16),
            pltpu.VMEM((parts, state, sub), BF16),
            pltpu.VMEM((parts, state, sub), BF16),
            pltpu.VMEM((n_head, 8, share), F32),
            pltpu.VMEM((n_head - 1, 8, share), F32),
            pltpu.VMEM((2 * pieces, 2 * share, piece), F32),
            pltpu.VMEM((2 * pieces, share, piece), BF16),
            pltpu.VMEM((2 * pieces, share, piece), BF16),
            pltpu.VMEM((pieces, share, piece), BF16),
            pltpu.VMEM((pieces, share, piece), BF16),
            dma((8,)),
            dma((3,)),
            dma((2,)),
            dma((parts, 2)),
            dma((parts, 2)),
            dma((n_head - 1, 2)),
            dma((2 * pieces, 2)),
            dma((pieces, 2)),
        ],
        compiler_params=pltpu.CompilerParams(
            collective_id=0, has_side_effects=True, vmem_limit_bytes=56 * 1024 * 1024
        ),
    )(
        doc_starts,
        step_raw,
        step_bias.reshape(1, -1),
        decay_rate.reshape(1, -1),
        skip_scale.reshape(1, -1),
        norm_gain,
        in_coeff,
        out_coeff,
        stream,
        gate_input,
        out_proj,
    )


def solution(mesh):
    in_specs = (
        P("seq", "head"),
        P("seq", "head"),
        P("seq", None),
        P("seq", None),
        P("head", "seq"),
        P("head"),
        P("head"),
        P("head"),
        P("head"),
        P("head", None),
        P(),
    )
    out_specs = P(("seq", "head"), None)
    body = functools.partial(local, mesh.shape["seq"], mesh.shape["head"])
    return jax.shard_map(body, mesh=mesh, in_specs=in_specs, out_specs=out_specs, check_vma=False)
```

profile of v0, /device:TPU:25, one launch (start us, length us, event | category | flops | bytes accessed | tf_op | source)
XLA Modules:
  0.0 45.8 jit_solution(15995437255643603888)
XLA Ops:
  0.0 43.8 %shard_map.109 = bf16[128,2560]{1,0:T(8,128)(2,1)} custom-call(s32[16]{0:T(128)} %starts_hbm.1, f32[20,512]{1,0:T(8,128)} %step_hbm.1, f32[1,20]{1,0:T(1,128)} %bitcast.3, f32[1,20]{1,0:T(1,128)} %bitcast.4, f32[1,20]{1,0:T(1,128)} %bitcast.5, f32[1280]{0:T(1024)} %gain_hbm.1, bf16[512,128]{1,0:T(8,128)(2,1)} %in_hbm.1, bf16[512,128]{1,0:T(8,128)(2,1)} %out_hbm.1, ...), custom_call_target="tpu_custom_call" | custom-call | tf_op jit(solution)/shard_map/pallas_call | solution.py:482
  43.8 2.0 %copy.13 = bf16[128,2560]{1,0:T(8,128)(2,1)} copy(bf16[128,2560]{1,0:T(8,128)(2,1)} %shard_map.109) | data formatting | bytes 1310720
where the time goes:
time: 45.9 us; the launch traced here: 45.8 us
  Pallas kernels  43.8 us (95%)
  local copies, waits for them, and re-layouts  1.97 us (4%)
    pallas_call x1, Pallas kernels, local(): pl.pallas_call(functools.partial(kernel, n_seq, n_head, heads, chunks, pi...  43.8 us
    unnamed x1, local copies, waits for them, and re-layouts  1.97 us

commit v1 on v0

--- a/solution.py
+++ b/solution.py
@@ -146,10 +146,16 @@
         small.start()
 
     barrier = pltpu.get_barrier_semaphore()
-    for step in (1, 2, n_seq - 2, n_seq - 1):
-        pl.semaphore_signal(barrier, inc=1, device_id=((s + step) % n_seq, g), device_id_type=MESH)
+    greeted = [(s >= 2, s - 2), (s >= 1, s - 1), (s + 1 < n_seq, s + 1), (s + 2 < n_seq, s + 2)]
+    for there, other in greeted:
+
+        @pl.when(there)
+        def _(other=other):
+            pl.semaphore_signal(barrier, inc=1, device_id=(other, g), device_id_type=MESH)
+
     for peer in peers:
         pl.semaphore_signal(barrier, inc=1, device_id=(s, peer), device_id_type=MESH)
+    greetings = len(peers) + sum(there.astype(jnp.int32) for there, _ in greeted)
 
     def send(src, dst, sems, seq, head):
         return pltpu.make_async_remote_copy(
@@ -212,7 +218,7 @@
     before_gate[1:2, :] = end_gate
     in_end = jnp.where(doc == doc_end, in_ref[...].astype(F32), 0.0).astype(BF16)
 
-    pl.semaphore_wait(barrier, 4 + len(peers))
+    pl.semaphore_wait(barrier, greetings)
 
     @pl.when(s < n_seq - 1)
     def _():
@@ -378,6 +384,17 @@
         far_out[j] = both.astype(BF16)
         far_copy(j).start()
 
+    def square_copy(i):
+        return send(square_out.at[peers[i]], square_in.at[i], square_sem.at[i], s, peers[i])
+
+    def send_squares():
+        for owner in range(n_head):
+            block = square[owner * share : (owner + 1) * share, :]
+            sums_lane = jnp.sum(block.T, axis=0, keepdims=True)
+            square_out[owner] = jnp.broadcast_to(sums_lane, (8, share))
+        for i in range(len(peers)):
+            square_copy(i).start()
+
     def far_step(j, _):
         @pl.when(j < pieces)
         def _():
@@ -387,16 +404,13 @@
         def _():
             pass_on(j - FAR_LAG)
 
+        @pl.when(j == FAR_LAG)
+        def _():
+            send_squares()
+
         return 0
 
     lax.fori_loop(0, pieces + FAR_LAG, far_step, 0)
-
-    for owner in range(n_head):
-        block = square[owner * share : (owner + 1) * share, :]
-        sums_lane = jnp.sum(block.T, axis=0, keepdims=True)
-        square_out[owner] = jnp.broadcast_to(sums_lane, (8, share))
-    for i, peer in enumerate(peers):
-        send(square_out.at[peer], square_in.at[i], square_sem.at[i], s, peer).start()
 
     def near_step(j, _):
         project(1, side, j)
@@ -405,8 +419,8 @@
     lax.fori_loop(0, pieces, near_step, 0)
 
     total = square_out[g]
-    for i, peer in enumerate(peers):
-        send(square_out.at[peer], square_in.at[i], square_sem.at[i], s, peer).wait()
+    for i in range(len(peers)):
+        square_copy(i).wait()
         total = total + square_in[i]
     mean = jnp.broadcast_to(total[0:1, :], (128, share)).T / (channels * n_head)
     scale_row = lax.rsqrt(mean + EPSILON)[:, 0:1]
@@ -481,7 +495,7 @@
     dma = pltpu.SemaphoreType.DMA
     return pl.pallas_call(
         functools.partial(kernel, n_seq, n_head, heads, chunks, pieces),
-        out_shape=jax.ShapeDtypeStruct((share, model), BF16),
+        out_shape=pltpu.VMEM((share, model), BF16),
         in_specs=[anywhere] * 11,
         out_specs=vmem,
         scratch_shapes=[

time: 45.9 us -> 40.1 us (0.87)
  Pallas kernels: 43.8 us -> 39.1 us
  local copies, waits for them, and re-layouts: 1.97 us -> 0.84 us
    pallas_call x1, Pallas kernels: 43.8 us -> 39.1 us  [local(): pl.pallas_call(functools.partial(kernel, n_seq, n_head, heads, chunks, pi...]
    unnamed x1, local copies, waits for them, and re-layouts: 1.97 us -> 0.84 us
where the time goes in v1:
time: 40.1 us; the launch traced here: 40 us
  Pallas kernels  39.1 us (98%)
  local copies, waits for them, and re-layouts  0.84 us (2%)
    pallas_call x1, Pallas kernels, local(): pl.pallas_call(functools.partial(kernel, n_seq, n_head, heads, chunks, pi...  39.1 us
    unnamed x1, local copies, waits for them, and re-layouts  0.84 us

profile of v1, /device:TPU:25, one launch (start us, length us, event | category | flops | bytes accessed | tf_op | source)
XLA Modules:
  0.0 40.0 jit_solution(15280106822590173495)
XLA Ops:
  0.0 39.1 %shard_map.109 = bf16[128,2560]{1,0:T(8,128)(2,1)S(1)} custom-call(s32[16]{0:T(128)} %starts_hbm.1, f32[20,512]{1,0:T(8,128)} %step_hbm.1, f32[1,20]{1,0:T(1,128)} %bitcast.3, f32[1,20]{1,0:T(1,128)} %bitcast.4, f32[1,20]{1,0:T(1,128)} %bitcast.5, f32[1280]{0:T(1024)} %gain_hbm.1, bf16[512,128]{1,0:T(8,128)(2,1)} %in_hbm.1, bf16[512,128]{1,0:T(8,128)(2,1)} %out_hbm.1, ...), custom_call_target="tpu_custom_call" | custom-call | tf_op jit(solution)/shard_map/pallas_call | solution.py:496
  39.1 0.8 %copy.13 = bf16[128,2560]{1,0:T(8,128)(2,1)} copy(bf16[128,2560]{1,0:T(8,128)(2,1)S(1)} %shard_map.109) | data formatting | bytes 1310720

commit v2 on v1

--- a/solution.py
+++ b/solution.py
@@ -11,8 +11,7 @@
 F32 = jnp.float32
 BF16 = jnp.bfloat16
 MESH = pl.DeviceIdType.MESH
-LAG = 2
-SPLIT = 2
+EARLY = 1
 FAR_LAG = 2
 
 
@@ -71,17 +70,18 @@
     pairs,
     carry_in,
     source,
-    summary,
     link_own,
-    link_prev,
+    link_all,
     before_gate,
     base,
     slope,
     square,
     hidden,
+    fresh_own,
+    fresh_all,
     chain_out,
-    chain_in,
-    cross_in,
+    states,
+    incoming_all,
     square_out,
     square_in,
     held,
@@ -91,9 +91,14 @@
     far_in,
     small_sem,
     load_sem,
-    link_sem,
+    ready_sem,
+    link_send,
+    link_recv,
+    fresh_send,
+    fresh_recv,
     chain_sem,
-    cross_sem,
+    return_send,
+    return_recv,
     square_sem,
     near_sem,
     far_sem,
@@ -103,7 +108,7 @@
     width = channels // chunks
     head_size = channels // heads
     padded = pad.shape[0]
-    sub = width // SPLIT
+    sub = width // 2
     half = rows // 2
     share = rows // n_head
     piece = proj.shape[1] // pieces
@@ -118,6 +123,8 @@
     near = side * 2 + (1 - core)
     far = (1 - side) * 2 + core
     cross = s + 1 - 2 * parity
+    carrier = 2 * side + 1
+    carries = core == 1
     peers = (near, far, (1 - side) * 2 + (1 - core))
 
     loads = [
@@ -146,41 +153,72 @@
         small.start()
 
     barrier = pltpu.get_barrier_semaphore()
-    greeted = [(s >= 2, s - 2), (s >= 1, s - 1), (s + 1 < n_seq, s + 1), (s + 2 < n_seq, s + 2)]
-    for there, other in greeted:
-
-        @pl.when(there)
-        def _(other=other):
-            pl.semaphore_signal(barrier, inc=1, device_id=(other, g), device_id_type=MESH)
-
     for peer in peers:
         pl.semaphore_signal(barrier, inc=1, device_id=(s, peer), device_id_type=MESH)
-    greetings = len(peers) + sum(there.astype(jnp.int32) for there, _ in greeted)
-
-    def send(src, dst, sems, seq, head):
+    for peer in (g, near):
+        pl.semaphore_signal(barrier, inc=1, device_id=(cross, peer), device_id_type=MESH)
+
+    @pl.when(pair < last_pair)
+    def _():
+        pl.semaphore_signal(barrier, inc=1, device_id=(s + 2, g), device_id_type=MESH)
+
+    def remote(src, dst, send_sem, recv_sem, seq, head):
         return pltpu.make_async_remote_copy(
             src_ref=src,
             dst_ref=dst,
-            send_sem=sems.at[0],
-            recv_sem=sems.at[1],
+            send_sem=send_sem,
+            recv_sem=recv_sem,
             device_id=(seq, head),
             device_id_type=MESH,
         )
 
-    link_copy = send(link_own, link_prev, link_sem, (s + 1) % n_seq, g)
-
-    def chain_copy(k):
+    def send(src, dst, sems, seq, head):
+        return remote(src, dst, sems.at[0], sems.at[1], seq, head)
+
+    def link_copy(away, shard, part):
+        return remote(
+            link_own,
+            link_all.at[shard, part],
+            link_send.at[away],
+            link_recv.at[shard, part],
+            cross if away else s,
+            carrier,
+        )
+
+    def fresh_copy(k, away, shard, part):
+        return remote(
+            fresh_own.at[k, 1 - parity if away else parity],
+            fresh_all.at[shard, part, k],
+            fresh_send.at[away, k],
+            fresh_recv.at[shard, part, k],
+            cross if away else s,
+            carrier,
+        )
+
+    def chain_copy(k, part):
         return send(
-            chain_out.at[k], chain_in.at[k], chain_sem.at[k], (s + 2) % n_seq, g
+            chain_out.at[k, part], states.at[0, k, part], chain_sem.at[k, part], (s + 2) % n_seq, g
         )
 
-    def cross_copy(k, even):
-        source_ref = chain_out if even else chain_in
-        return send(source_ref.at[k], cross_in.at[k], cross_sem.at[k], cross, g)
+    def return_copy(k, away, part, owner):
+        return remote(
+            states.at[1 - parity if away else parity, k, part],
+            incoming_all.at[k, owner],
+            return_send.at[k, away, part],
+            return_recv.at[k, owner],
+            cross if away else s,
+            2 * side + part,
+        )
 
     pad[...] = jnp.zeros_like(pad)
     for small in smalls:
         small.wait()
+    pl.semaphore_wait(barrier, len(peers) + 2 + (pair > 0).astype(jnp.int32))
+
+    @pl.when(carries & (pair > 0))
+    def _():
+        pl.semaphore_signal(ready_sem, inc=1, device_id=(s - 2, g), device_id_type=MESH)
+
     raw = step_ref[...] + to_column(bias_ref[...])
     pad[pl.ds(0, heads), :] = jnp.maximum(raw, 0.0) + jnp.log(1.0 + jnp.exp(-jnp.abs(raw)))
     step_size = pad[...]
@@ -218,11 +256,15 @@
     before_gate[1:2, :] = end_gate
     in_end = jnp.where(doc == doc_end, in_ref[...].astype(F32), 0.0).astype(BF16)
 
-    pl.semaphore_wait(barrier, greetings)
-
-    @pl.when(s < n_seq - 1)
-    def _():
-        link_copy.start()
+    link_copy(1, parity, core).start()
+
+    @pl.when(core == 0)
+    def _():
+        link_copy(0, parity, core).start()
+
+    @pl.when(carries)
+    def _():
+        link_all[parity, 1] = link_own[...]
 
     loads[0].wait()
     loads[1].start()
@@ -238,24 +280,17 @@
         source[:, cols] = scaled
         fresh = dot(in_end, scaled, 0, 0) * before_gate[1:2, cols]
 
-        @pl.when(pair == 0)
-        def _():
-            for i in range(SPLIT):
-                at = k * SPLIT + i
-                chain_out[at] = fresh[:, i * sub : (i + 1) * sub].astype(BF16)
-                chain_in[at] = jnp.zeros((state, sub), BF16)
-                if last_pair > 0:
-                    chain_copy(at).start()
-
-                @pl.when(parity == 0)
-                def _():
-                    cross_in[at] = jnp.zeros((state, sub), BF16)
-                    cross_copy(at, True).start()
-
-        @pl.when(pair > 0)
-        def _():
-            for i in range(SPLIT):
-                summary[k * SPLIT + i] = fresh[:, i * sub : (i + 1) * sub]
+        for i in range(2):
+            fresh_own[k, i] = fresh[:, i * sub : (i + 1) * sub].astype(BF16)
+        fresh_copy(k, 1, parity, core).start()
+
+        @pl.when(core == 0)
+        def _():
+            fresh_copy(k, 0, parity, core).start()
+
+        @pl.when(carries)
+        def _():
+            fresh_all[parity, 1, k] = fresh_own[k, parity]
 
         return 0
 
@@ -276,13 +311,15 @@
     square[...] = jnp.zeros_like(square)
     loads[1].wait()
 
-    @pl.when(s > 0)
-    def _():
-        link_copy.wait_recv()
-
     @pl.when(s == 0)
     def _():
-        link_prev[...] = jnp.zeros_like(link_prev)
+        incoming_all[...] = jnp.zeros_like(incoming_all)
+
+    @pl.when(carries)
+    def _():
+        link_copy(0, parity, 0).wait_recv()
+        link_copy(1, 1 - parity, 0).wait_recv()
+        link_copy(1, 1 - parity, 1).wait_recv()
 
     def local_part(k):
         cols = columns(k)
@@ -299,37 +336,55 @@
         slope[:, cols] = factor
         base[:, cols] = within * factor + stream[:, cols].astype(F32) * before_gate[2:3, cols] * silu
 
-    def forward(k):
-        @pl.when(pair > 0)
-        def _():
-            chain_copy(k).wait_recv()
-
-            @pl.when(parity == 1)
+    def chain_step(k):
+        cols = pl.ds(pl.multiple_of(k * width + parity * sub, sub), sub)
+        fresh_copy(k, 0, parity, 0).wait_recv()
+        fresh_copy(k, 1, 1 - parity, 0).wait_recv()
+        fresh_copy(k, 1, 1 - parity, 1).wait_recv()
+
+        for part in range(2):
+            keep_even, keep_odd = link_all[0, part, :, cols], link_all[1, part, :, cols]
+            fresh_even = fresh_all[0, part, k].astype(F32)
+            fresh_odd = fresh_all[1, part, k].astype(F32)
+
+            @pl.when(pair > 0)
             def _():
-                cross_copy(k, False).start()
-
-            cols = pl.ds(pl.multiple_of(k * sub, sub), sub)
-            longer = link_own[:, cols] * link_prev[:, cols] * chain_in[k].astype(F32)
-            chain_out[k] = (longer + summary[k]).astype(BF16)
+                chain_copy(k, part).wait_recv()
+                between = keep_even * states[0, k, part].astype(F32) + fresh_even
+                states[1, k, part] = between.astype(BF16)
+                chain_out[k, part] = (keep_odd * between + fresh_odd).astype(BF16)
+
+            @pl.when(pair == 0)
+            def _():
+                states[1, k, part] = fresh_all[0, part, k]
+                chain_out[k, part] = (keep_odd * fresh_even + fresh_odd).astype(BF16)
 
             @pl.when(pair < last_pair)
             def _():
-                chain_copy(k).start()
-
-            @pl.when(parity == 0)
+                chain_copy(k, part).start()
+
+            @pl.when(cross > 0)
             def _():
-                cross_copy(k, True).start()
+                return_copy(k, 1, part, parity).start()
+
+            @pl.when(s > 0)
+            def _():
+                if part == 0:
+                    return_copy(k, 0, part, parity).start()
+                else:
+                    incoming_all[k, parity] = states[parity, k, part]
 
     def finish(k):
         @pl.when(s > 0)
         def _():
-            for i in range(SPLIT):
-                cross_copy(k * SPLIT + i, True).wait_recv()
+            return_copy(k, 1, core, 1 - parity).wait_recv()
+
+            @pl.when(core == 0)
+            def _():
+                return_copy(k, 0, core, parity).wait_recv()
 
         cols = columns(k)
-        own = jnp.concatenate([chain_in[k * SPLIT + i].astype(F32) for i in range(SPLIT)], axis=1)
-        other = jnp.concatenate([cross_in[k * SPLIT + i].astype(F32) for i in range(SPLIT)], axis=1)
-        incoming = link_prev[:, cols] * own + other
+        incoming = jnp.concatenate([incoming_all[k, i].astype(F32) for i in range(2)], axis=1)
         incoming = (incoming * before_gate[0:1, cols]).astype(BF16)
         carried = dot(carry_in[...], incoming, 1, 0)
         gated = base[:, cols] + slope[:, cols] * carried
@@ -340,20 +395,30 @@
             total = total + squares[:, i * 128 : (i + 1) * 128]
         square[...] = total
 
-    def main_step(k, _):
-        @pl.when(k < chunks)
-        def _():
-            local_part(k)
-            for i in range(SPLIT):
-                forward(k * SPLIT + i)
-
-        @pl.when(k >= LAG)
-        def _():
-            finish(k - LAG)
-
-        return 0
-
-    lax.fori_loop(0, chunks + LAG, main_step, 0)
+    lead = jnp.where(carries & (pair < EARLY), 0, chunks)
+
+    def main_step(step, _):
+        @pl.when(carries & (step >= lead) & (step < lead + chunks))
+        def _():
+            chain_step(step - lead)
+
+        @pl.when(step < chunks)
+        def _():
+            local_part(step)
+
+        return 0
+
+    @pl.when(carries & (pair < last_pair))
+    def _():
+        pl.semaphore_wait(ready_sem, 1)
+
+    lax.fori_loop(0, chunks + jnp.where(carries, lead, 0), main_step, 0)
+
+    def finish_step(k, _):
+        finish(k)
+        return 0
+
+    lax.fori_loop(0, chunks, finish_step, 0)
 
     loads[2].wait()
 
@@ -435,26 +500,38 @@
 
     lax.fori_loop(0, pieces, collect, 0)
 
-    @pl.when(s < n_seq - 1)
-    def _():
-        link_copy.wait_send()
+    link_copy(1, parity, core).wait_send()
+
+    @pl.when(core == 0)
+    def _():
+        link_copy(0, parity, core).wait_send()
 
     def drain(k, _):
-        @pl.when(pair < last_pair)
-        def _():
-            chain_copy(k).wait_send()
-
-        @pl.when(parity == 0)
-        def _():
-            cross_copy(k, True).wait_send()
-
-        @pl.when((parity == 1) & (pair > 0))
-        def _():
-            cross_copy(k, False).wait_send()
-
-        return 0
-
-    lax.fori_loop(0, chunks * SPLIT, drain, 0)
+        fresh_copy(k, 1, parity, core).wait_send()
+
+        @pl.when(core == 0)
+        def _():
+            fresh_copy(k, 0, parity, core).wait_send()
+
+        @pl.when(carries)
+        def _():
+            for part in range(2):
+
+                @pl.when(pair < last_pair)
+                def _():
+                    chain_copy(k, part).wait_send()
+
+                @pl.when(cross > 0)
+                def _():
+                    return_copy(k, 1, part, parity).wait_send()
+
+            @pl.when(s > 0)
+            def _():
+                return_copy(k, 0, 0, parity).wait_send()
+
+        return 0
+
+    lax.fori_loop(0, chunks, drain, 0)
 
     def drain_pieces(j, _):
         near_copy(0, j).wait_send()
@@ -486,7 +563,7 @@
     model = out_proj.shape[1]
     chunks, pieces = channels // 256, model // 256
     width, piece = channels // chunks, model // pieces
-    parts, sub = chunks * SPLIT, width // SPLIT
+    sub = width // 2
     padded = -(-heads // 8) * 8
     share = rows // n_head
     assert n_head == 4 and n_seq % 2 == 0 and rows <= 512
@@ -517,17 +594,18 @@
             pltpu.VMEM((rows, rows), BF16),
             pltpu.VMEM((rows, state), BF16),
             pltpu.VMEM((rows, channels), BF16),
-            pltpu.VMEM((parts, state, sub), F32),
             pltpu.VMEM((1, channels), F32),
-            pltpu.VMEM((1, channels), F32),
+            pltpu.VMEM((2, 2, 1, channels), F32),
             pltpu.VMEM((8, channels), F32),
             pltpu.VMEM((rows, channels), F32),
             pltpu.VMEM((rows, channels), F32),
             pltpu.VMEM((rows, 128), F32),
             pltpu.VMEM((rows, channels), BF16),
-            pltpu.VMEM((parts, state, sub), BF16),
-            pltpu.VMEM((parts, state, sub), BF16),
-            pltpu.VMEM((parts, state, sub), BF16),
+            pltpu.VMEM((chunks, 2, state, sub), BF16),
+            pltpu.VMEM((2, 2, chunks, state, sub), BF16),
+            pltpu.VMEM((chunks, 2, state, sub), BF16),
+            pltpu.VMEM((2, chunks, 2, state, sub), BF16),
+            pltpu.VMEM((chunks, 2, state, sub), BF16),
             pltpu.VMEM((n_head, 8, share), F32),
             pltpu.VMEM((n_head - 1, 8, share), F32),
             pltpu.VMEM((2 * pieces, 2 * share, piece), F32),
@@ -537,9 +615,14 @@
             pltpu.VMEM((pieces, share, piece), BF16),
             dma((8,)),
             dma((3,)),
+            pltpu.SemaphoreType.REGULAR,
             dma((2,)),
-            dma((parts, 2)),
-            dma((parts, 2)),
+            dma((2, 2)),
+            dma((2, chunks)),
+            dma((2, 2, chunks)),
+            dma((chunks, 2, 2)),
+            dma((chunks, 2, 2)),
+            dma((chunks, 2)),
             dma((n_head - 1, 2)),
             dma((2 * pieces, 2)),
             dma((pieces, 2)),

time: 40.1 us -> 37.1 us (0.925)
  the two profiles are of different devices: /device:TPU:25 before, /device:TPU:24 now
where the time goes in v2:
time: 37.1 us; the launch traced here: 37 us
  Pallas kernels  36.1 us (97%)
  local copies, waits for them, and re-layouts  0.84 us (2%)
    pallas_call x1, Pallas kernels, local(): pl.pallas_call(functools.partial(kernel, n_seq, n_head, heads, chunks, pi...  36.1 us
    unnamed x1, local copies, waits for them, and re-layouts  0.84 us

profile of v2, /device:TPU:24, one launch (start us, length us, event | category | flops | bytes accessed | tf_op | source)
XLA Modules:
  0.0 37.0 jit_solution(2831138888326423573)
XLA Ops:
  0.0 36.1 %shard_map.109 = bf16[128,2560]{1,0:T(8,128)(2,1)S(1)} custom-call(s32[16]{0:T(128)} %starts_hbm.1, f32[20,512]{1,0:T(8,128)} %step_hbm.1, f32[1,20]{1,0:T(1,128)} %bitcast.3, f32[1,20]{1,0:T(1,128)} %bitcast.4, f32[1,20]{1,0:T(1,128)} %bitcast.5, f32[1280]{0:T(1024)} %gain_hbm.1, bf16[512,128]{1,0:T(8,128)(2,1)} %in_hbm.1, bf16[512,128]{1,0:T(8,128)(2,1)} %out_hbm.1, ...), custom_call_target="tpu_custom_call" | custom-call | tf_op jit(solution)/shard_map/pallas_call | solution.py:573
  36.2 0.8 %copy.13 = bf16[128,2560]{1,0:T(8,128)(2,1)} copy(bf16[128,2560]{1,0:T(8,128)(2,1)S(1)} %shard_map.109) | data formatting | bytes 1310720

commit v3 on v2

--- a/solution.py
+++ b/solution.py
@@ -13,6 +13,7 @@
 MESH = pl.DeviceIdType.MESH
 EARLY = 1
 FAR_LAG = 2
+LENT = (2, 1)
 
 
 def dot(a, b, ca, cb):
@@ -32,6 +33,12 @@
     n = row.shape[1]
     eye = lax.broadcasted_iota(jnp.int32, (n, n), 0) == lax.broadcasted_iota(jnp.int32, (n, n), 1)
     return jnp.sum(jnp.where(eye, row, 0.0), axis=1, keepdims=True)
+
+
+def lends(pair, last_pair):
+    if last_pair + 1 < 2 * len(LENT):
+        return 0 * pair
+    return sum(jnp.where(pair == last_pair - i, count, 0) for i, count in enumerate(LENT))
 
 
 def kernel(
@@ -89,6 +96,7 @@
     near_in,
     far_out,
     far_in,
+    relay_in,
     small_sem,
     load_sem,
     ready_sem,
@@ -96,12 +104,19 @@
     link_recv,
     fresh_send,
     fresh_recv,
-    chain_sem,
+    chain_send,
+    chain_recv,
     return_send,
     return_recv,
-    square_sem,
-    near_sem,
-    far_sem,
+    square_send,
+    square_recv,
+    near_send,
+    near_recv,
+    near_last,
+    far_send,
+    far_recv,
+    relay_send,
+    relay_recv,
 ):
     rows, channels = stream.shape
     state = in_ref.shape[1]
@@ -125,6 +140,10 @@
     cross = s + 1 - 2 * parity
     carrier = 2 * side + 1
     carries = core == 1
+    helped = last_pair - pair
+    lent = lends(pair, last_pair)
+    borrowed = lends(helped, last_pair)
+    helper = 2 * helped + parity
     peers = (near, far, (1 - side) * 2 + (1 - core))
 
     loads = [
@@ -146,10 +165,10 @@
             )
         )
     ]
-    for small in smalls[:3]:
+    for small in smalls[:5]:
         small.start()
     loads[0].start()
-    for small in smalls[3:]:
+    for small in smalls[5:]:
         small.start()
 
     barrier = pltpu.get_barrier_semaphore()
@@ -161,6 +180,10 @@
     @pl.when(pair < last_pair)
     def _():
         pl.semaphore_signal(barrier, inc=1, device_id=(s + 2, g), device_id_type=MESH)
+
+    @pl.when(borrowed > 0)
+    def _():
+        pl.semaphore_signal(barrier, inc=1, device_id=(helper, far), device_id_type=MESH)
 
     def remote(src, dst, send_sem, recv_sem, seq, head):
         return pltpu.make_async_remote_copy(
@@ -172,53 +195,58 @@
             device_id_type=MESH,
         )
 
-    def send(src, dst, sems, seq, head):
-        return remote(src, dst, sems.at[0], sems.at[1], seq, head)
-
-    def link_copy(away, shard, part):
+    def slot(part, away):
+        return 2 * part + 1 - away
+
+    def link_copy(away):
         return remote(
             link_own,
-            link_all.at[shard, part],
+            link_all.at[slot(core, away)],
             link_send.at[away],
-            link_recv.at[shard, part],
+            link_recv,
             cross if away else s,
             carrier,
         )
 
-    def fresh_copy(k, away, shard, part):
+    def fresh_copy(k, away):
         return remote(
             fresh_own.at[k, 1 - parity if away else parity],
-            fresh_all.at[shard, part, k],
-            fresh_send.at[away, k],
-            fresh_recv.at[shard, part, k],
+            fresh_all.at[k, slot(core, away)],
+            fresh_send.at[away],
+            fresh_recv.at[k],
             cross if away else s,
             carrier,
         )
 
     def chain_copy(k, part):
-        return send(
-            chain_out.at[k, part], states.at[0, k, part], chain_sem.at[k, part], (s + 2) % n_seq, g
+        return remote(
+            chain_out.at[k, part],
+            states.at[0, k, part],
+            chain_send,
+            chain_recv.at[k, part],
+            (s + 2) % n_seq,
+            g,
         )
 
     def return_copy(k, away, part, owner):
         return remote(
             states.at[1 - parity if away else parity, k, part],
             incoming_all.at[k, owner],
-            return_send.at[k, away, part],
+            return_send.at[away],
             return_recv.at[k, owner],
             cross if away else s,
             2 * side + part,
         )
 
+    def arrived(dst, sem):
+        remote(dst, dst, sem, sem, s, near).wait_recv()
+
+    def left(src, sem):
+        remote(src, src, sem, sem, s, near).wait_send()
+
     pad[...] = jnp.zeros_like(pad)
-    for small in smalls:
+    for small in smalls[:3]:
         small.wait()
-    pl.semaphore_wait(barrier, len(peers) + 2 + (pair > 0).astype(jnp.int32))
-
-    @pl.when(carries & (pair > 0))
-    def _():
-        pl.semaphore_signal(ready_sem, inc=1, device_id=(s - 2, g), device_id_type=MESH)
-
     raw = step_ref[...] + to_column(bias_ref[...])
     pad[pl.ds(0, heads), :] = jnp.maximum(raw, 0.0) + jnp.log(1.0 + jnp.exp(-jnp.abs(raw)))
     step_size = pad[...]
@@ -239,6 +267,8 @@
     last = cumulative[:, rows - 1 : rows]
     factor_in[...] = split(jnp.exp(middle - cumulative) * step_size, 2)
 
+    for small in smalls[3:5]:
+        small.wait()
     starts = starts_ref[...].astype(F32).reshape(1, -1)
     offset = s * rows
     place = (offset + lax.broadcasted_iota(jnp.int32, (rows, 1), 0)).astype(F32)
@@ -256,15 +286,22 @@
     before_gate[1:2, :] = end_gate
     in_end = jnp.where(doc == doc_end, in_ref[...].astype(F32), 0.0).astype(BF16)
 
-    link_copy(1, parity, core).start()
+    greetings = len(peers) + 2 + (pair > 0).astype(jnp.int32) + (lent > 0).astype(jnp.int32)
+    pl.semaphore_wait(barrier, greetings)
+
+    @pl.when(carries & (pair > 0))
+    def _():
+        pl.semaphore_signal(ready_sem, inc=1, device_id=(s - 2, g), device_id_type=MESH)
+
+    link_copy(1).start()
 
     @pl.when(core == 0)
     def _():
-        link_copy(0, parity, core).start()
+        link_copy(0).start()
 
     @pl.when(carries)
     def _():
-        link_all[parity, 1] = link_own[...]
+        link_all[3] = link_own[...]
 
     loads[0].wait()
     loads[1].start()
@@ -282,19 +319,22 @@
 
         for i in range(2):
             fresh_own[k, i] = fresh[:, i * sub : (i + 1) * sub].astype(BF16)
-        fresh_copy(k, 1, parity, core).start()
+        fresh_copy(k, 1).start()
 
         @pl.when(core == 0)
         def _():
-            fresh_copy(k, 0, parity, core).start()
+            fresh_copy(k, 0).start()
 
         @pl.when(carries)
         def _():
-            fresh_all[parity, 1, k] = fresh_own[k, parity]
+            fresh_all[k, 3] = fresh_own[k, parity]
 
         return 0
 
     lax.fori_loop(0, chunks, make_summary, 0)
+
+    for small in smalls[5:]:
+        small.wait()
 
     factor_out[...] = split(jnp.exp(cumulative - middle), 2)
     before_gate[3:4, :] = gain_ref[...].reshape(1, -1)
@@ -317,9 +357,7 @@
 
     @pl.when(carries)
     def _():
-        link_copy(0, parity, 0).wait_recv()
-        link_copy(1, 1 - parity, 0).wait_recv()
-        link_copy(1, 1 - parity, 1).wait_recv()
+        arrived(link_all.at[pl.ds(0, 3)], link_recv)
 
     def local_part(k):
         cols = columns(k)
@@ -338,14 +376,13 @@
 
     def chain_step(k):
         cols = pl.ds(pl.multiple_of(k * width + parity * sub, sub), sub)
-        fresh_copy(k, 0, parity, 0).wait_recv()
-        fresh_copy(k, 1, 1 - parity, 0).wait_recv()
-        fresh_copy(k, 1, 1 - parity, 1).wait_recv()
+        arrived(fresh_all.at[k, pl.ds(0, 3)], fresh_recv.at[k])
 
         for part in range(2):
-            keep_even, keep_odd = link_all[0, part, :, cols], link_all[1, part, :, cols]
-            fresh_even = fresh_all[0, part, k].astype(F32)
-            fresh_odd = fresh_all[1, part, k].astype(F32)
+            even, odd = 2 * part + 1 - parity, 2 * part + parity
+            keep_even, keep_odd = link_all[even, :, cols], link_all[odd, :, cols]
+            fresh_even = fresh_all[k, even].astype(F32)
+            fresh_odd = fresh_all[k, odd].astype(F32)
 
             @pl.when(pair > 0)
             def _():
@@ -356,7 +393,7 @@
 
             @pl.when(pair == 0)
             def _():
-                states[1, k, part] = fresh_all[0, part, k]
+                states[1, k, part] = fresh_all[k, even]
                 chain_out[k, part] = (keep_odd * fresh_even + fresh_odd).astype(BF16)
 
             @pl.when(pair < last_pair)
@@ -425,12 +462,22 @@
     def piece_columns(j):
         return pl.ds(pl.multiple_of(j * piece, piece), piece)
 
-    def near_copy(stage, j):
+    def near_copy(stage, j, sem):
         at = stage * pieces + j
-        return send(near_out.at[at], near_in.at[at], near_sem.at[at], s, near)
+        return remote(near_out.at[at], near_in.at[at], near_send, sem, s, near)
 
     def far_copy(j):
-        return send(far_out.at[j], far_in.at[j], far_sem.at[j], s, far)
+        return remote(far_out.at[j], far_in.at[j], far_send, far_recv.at[j], s, far)
+
+    def lend_copy(j):
+        return remote(
+            far_out.at[j], relay_in.at[j - 1], far_send, relay_recv.at[j - 1], helper, far
+        )
+
+    def relay_copy(i):
+        return remote(
+            relay_in.at[i], far_in.at[i + 1], relay_send.at[i], far_recv.at[i + 1], helper, g
+        )
 
     def half_rows(which):
         return pl.ds(pl.multiple_of(which * 2 * share, 2 * share), 2 * share)
@@ -441,16 +488,26 @@
     def project(stage, which, j):
         held[stage * pieces + j] = dot(hidden[half_rows(which), :], proj[:, piece_columns(j)], 1, 0)
         near_out[stage * pieces + j] = held[stage * pieces + j, core_rows(1 - core), :].astype(BF16)
-        near_copy(stage, j).start()
+        near_copy(stage, j, near_recv.at[j] if stage == 0 else near_last).start()
 
     def pass_on(j):
-        near_copy(0, j).wait_recv()
+        near_copy(0, j, near_recv.at[j]).wait_recv()
         both = held[j, core_rows(core), :] + near_in[j].astype(F32)
         far_out[j] = both.astype(BF16)
-        far_copy(j).start()
+        lend = (j >= 1) & (j <= lent)
+
+        @pl.when(lend)
+        def _():
+            lend_copy(j).start()
+
+        @pl.when(jnp.logical_not(lend))
+        def _():
+            far_copy(j).start()
 
     def square_copy(i):
-        return send(square_out.at[peers[i]], square_in.at[i], square_sem.at[i], s, peers[i])
+        return remote(
+            square_out.at[peers[i]], square_in.at[i], square_send, square_recv, s, peers[i]
+        )
 
     def send_squares():
         for owner in range(n_head):
@@ -483,15 +540,28 @@
 
     lax.fori_loop(0, pieces, near_step, 0)
 
+    def relay_step(i, _):
+        @pl.when(i < borrowed)
+        def _():
+            remote(
+                far_out.at[i + 1], relay_in.at[i], far_send, relay_recv.at[i], helper, far
+            ).wait_recv()
+            relay_copy(i).start()
+
+        return 0
+
+    lax.fori_loop(0, LENT[0], relay_step, 0)
+
+    arrived(square_in, square_recv)
     total = square_out[g]
     for i in range(len(peers)):
-        square_copy(i).wait()
         total = total + square_in[i]
     mean = jnp.broadcast_to(total[0:1, :], (128, share)).T / (channels * n_head)
     scale_row = lax.rsqrt(mean + EPSILON)[:, 0:1]
 
+    arrived(near_in.at[pl.ds(pieces, pieces)], near_last)
+
     def collect(j, _):
-        near_copy(1, j).wait_recv()
         far_copy(j).wait_recv()
         at = pieces + j
         whole = held[at, core_rows(core), :] + near_in[at].astype(F32) + far_in[j].astype(F32)
@@ -500,46 +570,38 @@
 
     lax.fori_loop(0, pieces, collect, 0)
 
-    link_copy(1, parity, core).wait_send()
+    link_copy(1).wait_send()
+    left(fresh_own.at[:, 0], fresh_send.at[1])
 
     @pl.when(core == 0)
     def _():
-        link_copy(0, parity, core).wait_send()
-
-    def drain(k, _):
-        fresh_copy(k, 1, parity, core).wait_send()
-
-        @pl.when(core == 0)
-        def _():
-            fresh_copy(k, 0, parity, core).wait_send()
-
-        @pl.when(carries)
-        def _():
-            for part in range(2):
-
-                @pl.when(pair < last_pair)
-                def _():
-                    chain_copy(k, part).wait_send()
-
-                @pl.when(cross > 0)
-                def _():
-                    return_copy(k, 1, part, parity).wait_send()
-
-            @pl.when(s > 0)
-            def _():
-                return_copy(k, 0, 0, parity).wait_send()
+        link_copy(0).wait_send()
+        left(fresh_own.at[:, 0], fresh_send.at[0])
+
+    @pl.when(carries & (pair < last_pair))
+    def _():
+        left(chain_out, chain_send)
+
+    @pl.when(carries & (cross > 0))
+    def _():
+        left(states.at[0], return_send.at[1])
+
+    @pl.when(carries & (s > 0))
+    def _():
+        left(states.at[0, :, 0], return_send.at[0])
+
+    left(square_out.at[pl.ds(0, 3)], square_send)
+    left(near_out, near_send)
+    left(far_out, far_send)
+
+    def drain_relay(i, _):
+        @pl.when(i < borrowed)
+        def _():
+            relay_copy(i).wait_send()
 
         return 0
 
-    lax.fori_loop(0, chunks, drain, 0)
-
-    def drain_pieces(j, _):
-        near_copy(0, j).wait_send()
-        near_copy(1, j).wait_send()
-        far_copy(j).wait_send()
-        return 0
-
-    lax.fori_loop(0, pieces, drain_pieces, 0)
+    lax.fori_loop(0, LENT[0], drain_relay, 0)
 
 
 def local(
@@ -595,14 +657,14 @@
             pltpu.VMEM((rows, state), BF16),
             pltpu.VMEM((rows, channels), BF16),
             pltpu.VMEM((1, channels), F32),
-            pltpu.VMEM((2, 2, 1, channels), F32),
+            pltpu.VMEM((4, 1, channels), F32),
             pltpu.VMEM((8, channels), F32),
             pltpu.VMEM((rows, channels), F32),
             pltpu.VMEM((rows, channels), F32),
             pltpu.VMEM((rows, 128), F32),
             pltpu.VMEM((rows, channels), BF16),
             pltpu.VMEM((chunks, 2, state, sub), BF16),
-            pltpu.VMEM((2, 2, chunks, state, sub), BF16),
+            pltpu.VMEM((chunks, 4, state, sub), BF16),
             pltpu.VMEM((chunks, 2, state, sub), BF16),
             pltpu.VMEM((2, chunks, 2, state, sub), BF16),
             pltpu.VMEM((chunks, 2, state, sub), BF16),
@@ -613,19 +675,27 @@
             pltpu.VMEM((2 * pieces, share, piece), BF16),
             pltpu.VMEM((pieces, share, piece), BF16),
             pltpu.VMEM((pieces, share, piece), BF16),
+            pltpu.VMEM((LENT[0], share, piece), BF16),
             dma((8,)),
             dma((3,)),
             pltpu.SemaphoreType.REGULAR,
             dma((2,)),
-            dma((2, 2)),
-            dma((2, chunks)),
-            dma((2, 2, chunks)),
-            dma((chunks, 2, 2)),
-            dma((chunks, 2, 2)),
+            dma,
+            dma((2,)),
+            dma((chunks,)),
+            dma,
             dma((chunks, 2)),
-            dma((n_head - 1, 2)),
-            dma((2 * pieces, 2)),
-            dma((pieces, 2)),
+            dma((2,)),
+            dma((chunks, 2)),
+            dma,
+            dma,
+            dma,
+            dma((pieces,)),
+            dma,
+            dma,
+            dma((pieces,)),
+            dma((LENT[0],)),
+            dma((LENT[0],)),
         ],
         compiler_params=pltpu.CompilerParams(
             collective_id=0, has_side_effects=True, vmem_limit_bytes=56 * 1024 * 1024

time: 37.1 us -> 33.6 us (0.906)
  the two profiles are of different devices: /device:TPU:24 before, /device:TPU:8 now
where the time goes in v3:
time: 33.6 us; the launch traced here: 33.5 us
  Pallas kernels  32.6 us (97%)
  local copies, waits for them, and re-layouts  0.84 us (2%)
    pallas_call x1, Pallas kernels, local(): pl.pallas_call(functools.partial(kernel, n_seq, n_head, heads, chunks, pi...  32.6 us
    unnamed x1, local copies, waits for them, and re-layouts  0.84 us

profile of v3, /device:TPU:8, one launch (start us, length us, event | category | flops | bytes accessed | tf_op | source)
XLA Modules:
  0.0 33.5 jit_solution(5710513629757125895)
XLA Ops:
  0.0 32.6 %shard_map.109 = bf16[128,2560]{1,0:T(8,128)(2,1)S(1)} custom-call(s32[16]{0:T(128)} %starts_hbm.1, f32[20,512]{1,0:T(8,128)} %step_hbm.1, f32[1,20]{1,0:T(1,128)} %bitcast.3, f32[1,20]{1,0:T(1,128)} %bitcast.4, f32[1,20]{1,0:T(1,128)} %bitcast.5, f32[1280]{0:T(1024)} %gain_hbm.1, bf16[512,128]{1,0:T(8,128)(2,1)} %in_hbm.1, bf16[512,128]{1,0:T(8,128)(2,1)} %out_hbm.1, ...), custom_call_target="tpu_custom_call" | custom-call | tf_op jit(solution)/shard_map/pallas_call | solution.py:635
  32.6 0.8 %copy.13 = bf16[128,2560]{1,0:T(8,128)(2,1)} copy(bf16[128,2560]{1,0:T(8,128)(2,1)S(1)} %shard_map.109) | data formatting | bytes 1310720

commit v4 on v3

--- a/solution.py
+++ b/solution.py
@@ -11,9 +11,14 @@
 F32 = jnp.float32
 BF16 = jnp.bfloat16
 MESH = pl.DeviceIdType.MESH
-EARLY = 1
+LEAD = 1
+LEND_FROM = 2
 FAR_LAG = 2
-LENT = (2, 1)
+READY = 2
+SOON = 1
+LAG = 3
+LENT = ((2, 2), (1, 0))
+SLOTS = max(max(counts) for counts in LENT)
 
 
 def dot(a, b, ca, cb):
@@ -35,10 +40,13 @@
     return jnp.sum(jnp.where(eye, row, 0.0), axis=1, keepdims=True)
 
 
-def lends(pair, last_pair):
+def lends(pair, last_pair, core):
     if last_pair + 1 < 2 * len(LENT):
         return 0 * pair
-    return sum(jnp.where(pair == last_pair - i, count, 0) for i, count in enumerate(LENT))
+    return sum(
+        jnp.where(pair == last_pair - i, jnp.where(core == 0, *counts), 0)
+        for i, counts in enumerate(LENT)
+    )
 
 
 def kernel(
@@ -97,6 +105,8 @@
     far_out,
     far_in,
     relay_in,
+    extra_out,
+    extra_in,
     small_sem,
     load_sem,
     ready_sem,
@@ -117,6 +127,8 @@
     far_recv,
     relay_send,
     relay_recv,
+    extra_send,
+    extra_recv,
 ):
     rows, channels = stream.shape
     state = in_ref.shape[1]
@@ -141,8 +153,8 @@
     carrier = 2 * side + 1
     carries = core == 1
     helped = last_pair - pair
-    lent = lends(pair, last_pair)
-    borrowed = lends(helped, last_pair)
+    lent = lends(pair, last_pair, core)
+    borrowed = lends(helped, last_pair, core)
     helper = 2 * helped + parity
     peers = (near, far, (1 - side) * 2 + (1 - core))
 
@@ -233,7 +245,7 @@
             states.at[1 - parity if away else parity, k, part],
             incoming_all.at[k, owner],
             return_send.at[away],
-            return_recv.at[k, owner],
+            return_recv.at[k],
             cross if away else s,
             2 * side + part,
         )
@@ -245,23 +257,24 @@
         remote(src, src, sem, sem, s, near).wait_send()
 
     pad[...] = jnp.zeros_like(pad)
+    head_row = lax.broadcasted_iota(jnp.int32, (padded, channels), 0) * head_size
+    lane = lax.broadcasted_iota(jnp.int32, (padded, channels), 1)
+    spread = jnp.where((lane >= head_row) & (lane < head_row + head_size), 1.0, 0.0)
+    expand[...] = jnp.concatenate([spread, spread], axis=0).astype(BF16)
+    first = lax.broadcasted_iota(jnp.int32, (rows, rows), 0)
+    second = lax.broadcasted_iota(jnp.int32, (rows, rows), 1)
+    upper = jnp.where(first <= second, 1.0, 0.0).astype(BF16)
+    pairs[...] = upper
     for small in smalls[:3]:
         small.wait()
     raw = step_ref[...] + to_column(bias_ref[...])
     pad[pl.ds(0, heads), :] = jnp.maximum(raw, 0.0) + jnp.log(1.0 + jnp.exp(-jnp.abs(raw)))
     step_size = pad[...]
-    head_row = lax.broadcasted_iota(jnp.int32, (padded, channels), 0) * head_size
-    lane = lax.broadcasted_iota(jnp.int32, (padded, channels), 1)
-    spread = jnp.where((lane >= head_row) & (lane < head_row + head_size), 1.0, 0.0)
-    expand[...] = jnp.concatenate([spread, spread], axis=0).astype(BF16)
     rate = to_column(rate_ref[...])
     if padded > heads:
         rate = jnp.concatenate([rate, jnp.zeros((padded - heads, 1), F32)], axis=0)
     log_decay = -step_size * rate
-    first = lax.broadcasted_iota(jnp.int32, (rows, rows), 0)
-    second = lax.broadcasted_iota(jnp.int32, (rows, rows), 1)
-    upper = jnp.where(first <= second, 1.0, 0.0).astype(BF16)
-    sums = dot(split(log_decay, 3), upper, 1, 0)
+    sums = dot(split(log_decay, 3), pairs[...], 1, 0)
     cumulative = sums[:padded] + sums[padded : 2 * padded] + sums[2 * padded :]
     middle = cumulative[:, half - 1 : half]
     last = cumulative[:, rows - 1 : rows]
@@ -286,29 +299,30 @@
     before_gate[1:2, :] = end_gate
     in_end = jnp.where(doc == doc_end, in_ref[...].astype(F32), 0.0).astype(BF16)
 
-    greetings = len(peers) + 2 + (pair > 0).astype(jnp.int32) + (lent > 0).astype(jnp.int32)
-    pl.semaphore_wait(barrier, greetings)
-
-    @pl.when(carries & (pair > 0))
-    def _():
-        pl.semaphore_signal(ready_sem, inc=1, device_id=(s - 2, g), device_id_type=MESH)
-
-    link_copy(1).start()
-
-    @pl.when(core == 0)
-    def _():
-        link_copy(0).start()
-
-    @pl.when(carries)
-    def _():
-        link_all[3] = link_own[...]
-
     loads[0].wait()
     loads[1].start()
     loads[2].start()
 
     def columns(k):
         return pl.ds(pl.multiple_of(k * width, width), width)
+
+    def meet():
+        greetings = len(peers) + 2 + (pair > 0).astype(jnp.int32) + (lent > 0).astype(jnp.int32)
+        pl.semaphore_wait(barrier, greetings)
+
+        @pl.when(carries & (pair > 0))
+        def _():
+            pl.semaphore_signal(ready_sem, inc=1, device_id=(s - 2, g), device_id_type=MESH)
+
+        link_copy(1).start()
+
+        @pl.when(core == 0)
+        def _():
+            link_copy(0).start()
+
+        @pl.when(carries)
+        def _():
+            link_all[3] = link_own[...]
 
     def make_summary(k, _):
         cols = columns(k)
@@ -319,6 +333,10 @@
 
         for i in range(2):
             fresh_own[k, i] = fresh[:, i * sub : (i + 1) * sub].astype(BF16)
+        @pl.when(k == 0)
+        def _():
+            meet()
+
         fresh_copy(k, 1).start()
 
         @pl.when(core == 0)
@@ -411,28 +429,42 @@
                 else:
                     incoming_all[k, parity] = states[parity, k, part]
 
-    def finish(k):
-        @pl.when(s > 0)
-        def _():
-            return_copy(k, 1, core, 1 - parity).wait_recv()
-
-            @pl.when(core == 0)
-            def _():
-                return_copy(k, 0, core, parity).wait_recv()
-
+    def take(k):
+        @pl.when(carries & (s > 0))
+        def _():
+            arrived(incoming_all.at[k, 0], return_recv.at[k])
+
+        @pl.when((core == 0) & (s > 0))
+        def _():
+            arrived(incoming_all.at[k], return_recv.at[k])
+
+    def half_rows(which):
+        return pl.ds(pl.multiple_of(which * half, half), half)
+
+    def piece_columns(j):
+        return pl.ds(pl.multiple_of(j * piece, piece), piece)
+
+    def finish(k, span):
         cols = columns(k)
         incoming = jnp.concatenate([incoming_all[k, i].astype(F32) for i in range(2)], axis=1)
         incoming = (incoming * before_gate[0:1, cols]).astype(BF16)
-        carried = dot(carry_in[...], incoming, 1, 0)
-        gated = base[:, cols] + slope[:, cols] * carried
-        hidden[:, cols] = (gated * before_gate[3:4, cols]).astype(BF16)
+        carried = dot(carry_in[span, :], incoming, 1, 0)
+        gated = base[span, cols] + slope[span, cols] * carried
+        hidden[span, cols] = (gated * before_gate[3:4, cols]).astype(BF16)
         squares = gated * gated
-        total = square[...]
+        total = square[span, :]
         for i in range(width // 128):
             total = total + squares[:, i * 128 : (i + 1) * 128]
-        square[...] = total
-
-    lead = jnp.where(carries & (pair < EARLY), 0, chunks)
+        square[span, :] = total
+
+    def product(span, depth, j):
+        return dot(hidden[span, depth], proj[depth, piece_columns(j)], 1, 0)
+
+    early_depth = pl.ds(0, channels - width)
+    late_depth = pl.ds(channels - width, width)
+
+    lead = jnp.where(pair == 0, LEAD, chunks)
+
 
     def main_step(step, _):
         @pl.when(carries & (step >= lead) & (step < lead + chunks))
@@ -443,6 +475,11 @@
         def _():
             local_part(step)
 
+        @pl.when(carries & (step >= lead + LAG))
+        def _():
+            take(step - lead - LAG)
+            finish(step - lead - LAG, pl.ds(0, rows))
+
         return 0
 
     @pl.when(carries & (pair < last_pair))
@@ -451,16 +488,18 @@
 
     lax.fori_loop(0, chunks + jnp.where(carries, lead, 0), main_step, 0)
 
+    loads[2].wait()
+
     def finish_step(k, _):
-        finish(k)
+        take(k)
+        finish(k, pl.ds(0, rows))
         return 0
 
-    lax.fori_loop(0, chunks, finish_step, 0)
-
-    loads[2].wait()
-
-    def piece_columns(j):
-        return pl.ds(pl.multiple_of(j * piece, piece), piece)
+    lax.fori_loop(jnp.where(carries, chunks - LAG, 0), chunks - 1, finish_step, 0)
+    for j in range(READY):
+        held[j] = product(half_rows(1 - side), early_depth, j)
+    take(chunks - 1)
+    finish(chunks - 1, half_rows(1 - side))
 
     def near_copy(stage, j, sem):
         at = stage * pieces + j
@@ -471,30 +510,49 @@
 
     def lend_copy(j):
         return remote(
-            far_out.at[j], relay_in.at[j - 1], far_send, relay_recv.at[j - 1], helper, far
+            far_out.at[j],
+            relay_in.at[j - LEND_FROM],
+            far_send,
+            relay_recv.at[j - LEND_FROM],
+            helper,
+            far,
         )
 
     def relay_copy(i):
         return remote(
-            relay_in.at[i], far_in.at[i + 1], relay_send.at[i], far_recv.at[i + 1], helper, g
-        )
-
-    def half_rows(which):
-        return pl.ds(pl.multiple_of(which * 2 * share, 2 * share), 2 * share)
+            relay_in.at[i],
+            far_in.at[i + LEND_FROM],
+            relay_send.at[i],
+            far_recv.at[i + LEND_FROM],
+            helper,
+            g,
+        )
 
     def core_rows(which):
         return pl.ds(pl.multiple_of(which * share, share), share)
 
+    def extra_copy():
+        return remote(extra_out, extra_in, extra_send, extra_recv, s, near)
+
+    def extra_far_copy():
+        return remote(
+            extra_out, far_in.at[pieces - 1], extra_send, far_recv.at[pieces - 1], s, 2 * (1 - side)
+        )
+
+    def exchange(stage, j):
+        at = stage * pieces + j
+        near_out[at] = held[at, core_rows(1 - core), :].astype(BF16)
+        near_copy(stage, j, near_recv.at[j] if stage == 0 else near_last).start()
+
     def project(stage, which, j):
-        held[stage * pieces + j] = dot(hidden[half_rows(which), :], proj[:, piece_columns(j)], 1, 0)
-        near_out[stage * pieces + j] = held[stage * pieces + j, core_rows(1 - core), :].astype(BF16)
-        near_copy(stage, j, near_recv.at[j] if stage == 0 else near_last).start()
+        at = stage * pieces + j
+        held[at] = product(half_rows(which), pl.ds(0, channels), j)
 
     def pass_on(j):
         near_copy(0, j, near_recv.at[j]).wait_recv()
         both = held[j, core_rows(core), :] + near_in[j].astype(F32)
         far_out[j] = both.astype(BF16)
-        lend = (j >= 1) & (j <= lent)
+        lend = (j >= LEND_FROM) & (j < LEND_FROM + lent)
 
         @pl.when(lend)
         def _():
@@ -503,6 +561,12 @@
         @pl.when(jnp.logical_not(lend))
         def _():
             far_copy(j).start()
+
+    def pass_on_extra():
+        extra_copy().wait_recv()
+        both = held[pieces - 1, core_rows(1 - core), :] + extra_in[...].astype(F32)
+        extra_out[...] = both.astype(BF16)
+        extra_far_copy().start()
 
     def square_copy(i):
         return remote(
@@ -518,17 +582,36 @@
             square_copy(i).start()
 
     def far_step(j, _):
-        @pl.when(j < pieces)
+        @pl.when(j < READY)
+        def _():
+            held[j] = held[j] + product(half_rows(1 - side), late_depth, j)
+
+        @pl.when((j >= READY) & (j < pieces))
         def _():
             project(0, 1 - side, j)
 
-        @pl.when(j >= FAR_LAG)
+        @pl.when((j < pieces - 1) | ((j == pieces - 1) & (core == 0)))
+        def _():
+            exchange(0, j)
+
+        @pl.when((j == pieces - 1) & (core == 0))
+        def _():
+            extra_out[...] = held[pieces - 1, core_rows(core), :].astype(BF16)
+            extra_copy().start()
+
+        @pl.when(j == SOON)
+        def _():
+            pass_on(0)
+            finish(chunks - 1, half_rows(side))
+            send_squares()
+
+        @pl.when(carries & (j == pieces + FAR_LAG - 1))
+        def _():
+            pass_on_extra()
+
+        @pl.when((j > FAR_LAG) & (carries | (j < pieces + FAR_LAG - 1)))
         def _():
             pass_on(j - FAR_LAG)
-
-        @pl.when(j == FAR_LAG)
-        def _():
-            send_squares()
 
         return 0
 
@@ -536,6 +619,7 @@
 
     def near_step(j, _):
         project(1, side, j)
+        exchange(1, j)
         return 0
 
     lax.fori_loop(0, pieces, near_step, 0)
@@ -544,13 +628,13 @@
         @pl.when(i < borrowed)
         def _():
             remote(
-                far_out.at[i + 1], relay_in.at[i], far_send, relay_recv.at[i], helper, far
+                far_out.at[i], relay_in.at[i], far_send, relay_recv.at[i], helper, far
             ).wait_recv()
             relay_copy(i).start()
 
         return 0
 
-    lax.fori_loop(0, LENT[0], relay_step, 0)
+    lax.fori_loop(0, SLOTS, relay_step, 0)
 
     arrived(square_in, square_recv)
     total = square_out[g]
@@ -591,8 +675,18 @@
         left(states.at[0, :, 0], return_send.at[0])
 
     left(square_out.at[pl.ds(0, 3)], square_send)
-    left(near_out, near_send)
-    left(far_out, far_send)
+
+    @pl.when(core == 0)
+    def _():
+        left(near_out, near_send)
+        left(far_out.at[pl.ds(0, pieces - 1)], far_send)
+
+    @pl.when(carries)
+    def _():
+        left(near_out.at[pl.ds(0, 2 * pieces - 1)], near_send)
+        left(far_out, far_send)
+
+    left(extra_out, extra_send)
 
     def drain_relay(i, _):
         @pl.when(i < borrowed)
@@ -601,7 +695,7 @@
 
         return 0
 
-    lax.fori_loop(0, LENT[0], drain_relay, 0)
+    lax.fori_loop(0, SLOTS, drain_relay, 0)
 
 
 def local(
@@ -675,7 +769,9 @@
             pltpu.VMEM((2 * pieces, share, piece), BF16),
             pltpu.VMEM((pieces, share, piece), BF16),
             pltpu.VMEM((pieces, share, piece), BF16),
-            pltpu.VMEM((LENT[0], share, piece), BF16),
+            pltpu.VMEM((SLOTS, share, piece), BF16),
+            pltpu.VMEM((share, piece), BF16),
+            pltpu.VMEM((share, piece), BF16),
             dma((8,)),
             dma((3,)),
             pltpu.SemaphoreType.REGULAR,
@@ -686,7 +782,7 @@
             dma,
             dma((chunks, 2)),
             dma((2,)),
-            dma((chunks, 2)),
+            dma((chunks,)),
             dma,
             dma,
             dma,
@@ -694,8 +790,10 @@
             dma,
             dma,
             dma((pieces,)),
-            dma((LENT[0],)),
-            dma((LENT[0],)),
+            dma((SLOTS,)),
+            dma((SLOTS,)),
+            dma,
+            dma,
         ],
         compiler_params=pltpu.CompilerParams(
             collective_id=0, has_side_effects=True, vmem_limit_bytes=56 * 1024 * 1024

time: 33.6 us -> 33.1 us (0.985)
  the two profiles are of different devices: /device:TPU:8 before, /device:TPU:17 now
where the time goes in v4:
time: 33.1 us; the launch traced here: 33 us
  Pallas kernels  32.1 us (97%)
  local copies, waits for them, and re-layouts  0.84 us (3%)
    pallas_call x1, Pallas kernels, local(): pl.pallas_call(functools.partial(kernel, n_seq, n_head, heads, chunks, pi...  32.1 us
    unnamed x1, local copies, waits for them, and re-layouts  0.84 us

profile of v4, /device:TPU:17, one launch (start us, length us, event | category | flops | bytes accessed | tf_op | source)
XLA Modules:
  0.0 33.0 jit_solution(15251740671980399384)
XLA Ops:
  0.0 32.1 %shard_map.109 = bf16[128,2560]{1,0:T(8,128)(2,1)S(1)} custom-call(s32[16]{0:T(128)} %starts_hbm.1, f32[20,512]{1,0:T(8,128)} %step_hbm.1, f32[1,20]{1,0:T(1,128)} %bitcast.3, f32[1,20]{1,0:T(1,128)} %bitcast.4, f32[1,20]{1,0:T(1,128)} %bitcast.5, f32[1280]{0:T(1024)} %gain_hbm.1, bf16[512,128]{1,0:T(8,128)(2,1)} %in_hbm.1, bf16[512,128]{1,0:T(8,128)(2,1)} %out_hbm.1, ...), custom_call_target="tpu_custom_call" | custom-call | tf_op jit(solution)/shard_map/pallas_call | solution.py:729
  32.1 0.8 %copy.13 = bf16[128,2560]{1,0:T(8,128)(2,1)} copy(bf16[128,2560]{1,0:T(8,128)(2,1)S(1)} %shard_map.109) | data formatting | bytes 1310720

commit v5 on v4

--- a/solution.py
+++ b/solution.py
@@ -100,12 +100,10 @@
     square_out,
     square_in,
     held,
-    near_out,
+    outbox,
     near_in,
-    far_out,
     far_in,
     relay_in,
-    extra_out,
     extra_in,
     small_sem,
     load_sem,
@@ -120,14 +118,12 @@
     return_recv,
     square_send,
     square_recv,
-    near_send,
+    sent,
     near_recv,
     near_last,
-    far_send,
     far_recv,
     relay_send,
     relay_recv,
-    extra_send,
     extra_recv,
 ):
     rows, channels = stream.shape
@@ -224,7 +220,7 @@
         return remote(
             fresh_own.at[k, 1 - parity if away else parity],
             fresh_all.at[k, slot(core, away)],
-            fresh_send.at[away],
+            fresh_send,
             fresh_recv.at[k],
             cross if away else s,
             carrier,
@@ -265,7 +261,7 @@
     second = lax.broadcasted_iota(jnp.int32, (rows, rows), 1)
     upper = jnp.where(first <= second, 1.0, 0.0).astype(BF16)
     pairs[...] = upper
-    for small in smalls[:3]:
+    for small in smalls[:5]:
         small.wait()
     raw = step_ref[...] + to_column(bias_ref[...])
     pad[pl.ds(0, heads), :] = jnp.maximum(raw, 0.0) + jnp.log(1.0 + jnp.exp(-jnp.abs(raw)))
@@ -280,8 +276,6 @@
     last = cumulative[:, rows - 1 : rows]
     factor_in[...] = split(jnp.exp(middle - cumulative) * step_size, 2)
 
-    for small in smalls[3:5]:
-        small.wait()
     starts = starts_ref[...].astype(F32).reshape(1, -1)
     offset = s * rows
     place = (offset + lax.broadcasted_iota(jnp.int32, (rows, 1), 0)).astype(F32)
@@ -333,7 +327,7 @@
 
         for i in range(2):
             fresh_own[k, i] = fresh[:, i * sub : (i + 1) * sub].astype(BF16)
-        @pl.when(k == 0)
+        @pl.when((k == 0) & carries)
         def _():
             meet()
 
@@ -348,6 +342,10 @@
             fresh_all[k, 3] = fresh_own[k, parity]
 
         return 0
+
+    @pl.when(core == 0)
+    def _():
+        meet()
 
     lax.fori_loop(0, chunks, make_summary, 0)
 
@@ -373,10 +371,6 @@
     def _():
         incoming_all[...] = jnp.zeros_like(incoming_all)
 
-    @pl.when(carries)
-    def _():
-        arrived(link_all.at[pl.ds(0, 3)], link_recv)
-
     def local_part(k):
         cols = columns(k)
         gate_value = gate[:, cols].astype(F32)
@@ -394,6 +388,11 @@
 
     def chain_step(k):
         cols = pl.ds(pl.multiple_of(k * width + parity * sub, sub), sub)
+
+        @pl.when(k == 0)
+        def _():
+            arrived(link_all.at[pl.ds(0, 3)], link_recv)
+
         arrived(fresh_all.at[k, pl.ds(0, 3)], fresh_recv.at[k])
 
         for part in range(2):
@@ -503,16 +502,19 @@
 
     def near_copy(stage, j, sem):
         at = stage * pieces + j
-        return remote(near_out.at[at], near_in.at[at], near_send, sem, s, near)
+        return remote(outbox.at[at], near_in.at[at], sent, sem, s, near)
+
+    def place(j):
+        return jnp.maximum(j - (pieces - 5), 0)
 
     def far_copy(j):
-        return remote(far_out.at[j], far_in.at[j], far_send, far_recv.at[j], s, far)
+        return remote(outbox.at[2 * pieces + j], far_in.at[j], sent, far_recv.at[place(j)], s, far)
 
     def lend_copy(j):
         return remote(
-            far_out.at[j],
+            outbox.at[2 * pieces + j],
             relay_in.at[j - LEND_FROM],
-            far_send,
+            sent,
             relay_recv.at[j - LEND_FROM],
             helper,
             far,
@@ -522,8 +524,8 @@
         return remote(
             relay_in.at[i],
             far_in.at[i + LEND_FROM],
-            relay_send.at[i],
-            far_recv.at[i + LEND_FROM],
+            relay_send,
+            far_recv.at[place(i + LEND_FROM)],
             helper,
             g,
         )
@@ -532,16 +534,16 @@
         return pl.ds(pl.multiple_of(which * share, share), share)
 
     def extra_copy():
-        return remote(extra_out, extra_in, extra_send, extra_recv, s, near)
+        return remote(outbox.at[3 * pieces], extra_in, sent, extra_recv, s, near)
 
     def extra_far_copy():
         return remote(
-            extra_out, far_in.at[pieces - 1], extra_send, far_recv.at[pieces - 1], s, 2 * (1 - side)
+            outbox.at[3 * pieces], far_in.at[pieces - 1], sent, far_recv.at[4], s, 2 * (1 - side)
         )
 
     def exchange(stage, j):
         at = stage * pieces + j
-        near_out[at] = held[at, core_rows(1 - core), :].astype(BF16)
+        outbox[at] = held[at, core_rows(1 - core), :].astype(BF16)
         near_copy(stage, j, near_recv.at[j] if stage == 0 else near_last).start()
 
     def project(stage, which, j):
@@ -551,7 +553,7 @@
     def pass_on(j):
         near_copy(0, j, near_recv.at[j]).wait_recv()
         both = held[j, core_rows(core), :] + near_in[j].astype(F32)
-        far_out[j] = both.astype(BF16)
+        outbox[2 * pieces + j] = both.astype(BF16)
         lend = (j >= LEND_FROM) & (j < LEND_FROM + lent)
 
         @pl.when(lend)
@@ -565,7 +567,7 @@
     def pass_on_extra():
         extra_copy().wait_recv()
         both = held[pieces - 1, core_rows(1 - core), :] + extra_in[...].astype(F32)
-        extra_out[...] = both.astype(BF16)
+        outbox[3 * pieces] = both.astype(BF16)
         extra_far_copy().start()
 
     def square_copy(i):
@@ -577,7 +579,7 @@
         for owner in range(n_head):
             block = square[owner * share : (owner + 1) * share, :]
             sums_lane = jnp.sum(block.T, axis=0, keepdims=True)
-            square_out[owner] = jnp.broadcast_to(sums_lane, (8, share))
+            square_out[owner] = sums_lane
         for i in range(len(peers)):
             square_copy(i).start()
 
@@ -596,7 +598,7 @@
 
         @pl.when((j == pieces - 1) & (core == 0))
         def _():
-            extra_out[...] = held[pieces - 1, core_rows(core), :].astype(BF16)
+            outbox[3 * pieces] = held[pieces - 1, core_rows(core), :].astype(BF16)
             extra_copy().start()
 
         @pl.when(j == SOON)
@@ -627,9 +629,7 @@
     def relay_step(i, _):
         @pl.when(i < borrowed)
         def _():
-            remote(
-                far_out.at[i], relay_in.at[i], far_send, relay_recv.at[i], helper, far
-            ).wait_recv()
+            arrived(relay_in.at[i], relay_recv.at[i])
             relay_copy(i).start()
 
         return 0
@@ -640,13 +640,18 @@
     total = square_out[g]
     for i in range(len(peers)):
         total = total + square_in[i]
-    mean = jnp.broadcast_to(total[0:1, :], (128, share)).T / (channels * n_head)
+    mean = jnp.broadcast_to(total, (128, share)).T / (channels * n_head)
     scale_row = lax.rsqrt(mean + EPSILON)[:, 0:1]
 
     arrived(near_in.at[pl.ds(pieces, pieces)], near_last)
 
+    arrived(far_in.at[pl.ds(0, pieces - 4)], far_recv.at[0])
+
     def collect(j, _):
-        far_copy(j).wait_recv()
+        @pl.when(j > pieces - 5)
+        def _():
+            far_copy(j).wait_recv()
+
         at = pieces + j
         whole = held[at, core_rows(core), :] + near_in[at].astype(F32) + far_in[j].astype(F32)
         result_ref[:, piece_columns(j)] = (whole * scale_row).astype(BF16)
@@ -655,12 +660,15 @@
     lax.fori_loop(0, pieces, collect, 0)
 
     link_copy(1).wait_send()
-    left(fresh_own.at[:, 0], fresh_send.at[1])
 
     @pl.when(core == 0)
     def _():
         link_copy(0).wait_send()
-        left(fresh_own.at[:, 0], fresh_send.at[0])
+        left(fresh_own, fresh_send)
+
+    @pl.when(carries)
+    def _():
+        left(fresh_own.at[:, 0], fresh_send)
 
     @pl.when(carries & (pair < last_pair))
     def _():
@@ -675,27 +683,13 @@
         left(states.at[0, :, 0], return_send.at[0])
 
     left(square_out.at[pl.ds(0, 3)], square_send)
-
-    @pl.when(core == 0)
-    def _():
-        left(near_out, near_send)
-        left(far_out.at[pl.ds(0, pieces - 1)], far_send)
-
-    @pl.when(carries)
-    def _():
-        left(near_out.at[pl.ds(0, 2 * pieces - 1)], near_send)
-        left(far_out, far_send)
-
-    left(extra_out, extra_send)
-
-    def drain_relay(i, _):
-        @pl.when(i < borrowed)
-        def _():
-            relay_copy(i).wait_send()
-
-        return 0
-
-    lax.fori_loop(0, SLOTS, drain_relay, 0)
+    left(outbox.at[pl.ds(0, 3 * pieces)], sent)
+
+    for count in range(1, SLOTS + 1):
+
+        @pl.when(borrowed == count)
+        def _():
+            left(relay_in.at[pl.ds(0, count)], relay_send)
 
 
 def local(
@@ -762,22 +756,20 @@
             pltpu.VMEM((chunks, 2, state, sub), BF16),
             pltpu.VMEM((2, chunks, 2, state, sub), BF16),
             pltpu.VMEM((chunks, 2, state, sub), BF16),
-            pltpu.VMEM((n_head, 8, share), F32),
-            pltpu.VMEM((n_head - 1, 8, share), F32),
+            pltpu.VMEM((n_head, 1, share), F32),
+            pltpu.VMEM((n_head - 1, 1, share), F32),
             pltpu.VMEM((2 * pieces, 2 * share, piece), F32),
-            pltpu.VMEM((2 * pieces, share, piece), BF16),
+            pltpu.VMEM((3 * pieces + 1, share, piece), BF16),
             pltpu.VMEM((2 * pieces, share, piece), BF16),
             pltpu.VMEM((pieces, share, piece), BF16),
-            pltpu.VMEM((pieces, share, piece), BF16),
             pltpu.VMEM((SLOTS, share, piece), BF16),
-            pltpu.VMEM((share, piece), BF16),
             pltpu.VMEM((share, piece), BF16),
             dma((8,)),
             dma((3,)),
             pltpu.SemaphoreType.REGULAR,
             dma((2,)),
             dma,
-            dma((2,)),
+            dma,
             dma((chunks,)),
             dma,
             dma((chunks, 2)),
@@ -788,11 +780,9 @@
             dma,
             dma((pieces,)),
             dma,
+            dma((5,)),
             dma,
-            dma((pieces,)),
             dma((SLOTS,)),
-            dma((SLOTS,)),
-            dma,
             dma,
         ],
         compiler_params=pltpu.CompilerParams(

time: 33.1 us -> 32.8 us (level)
    pallas_call x1, Pallas kernels: 32.1 us -> 31.8 us  [local(): pl.pallas_call(functools.partial(kernel, n_seq, n_head, heads, chunks, pi...]
where the time goes in v5:
time: 32.8 us; the launch traced here: 32.6 us
  Pallas kernels  31.8 us (97%)
  local copies, waits for them, and re-layouts  0.84 us (3%)
    pallas_call x1, Pallas kernels, local(): pl.pallas_call(functools.partial(kernel, n_seq, n_head, heads, chunks, pi...  31.8 us
    unnamed x1, local copies, waits for them, and re-layouts  0.84 us

profile of v5, /device:TPU:17, one launch (start us, length us, event | category | flops | bytes accessed | tf_op | source)
XLA Modules:
  0.0 32.6 jit_solution(7646136818287958298)
XLA Ops:
  0.0 31.8 %shard_map.109 = bf16[128,2560]{1,0:T(8,128)(2,1)S(1)} custom-call(s32[16]{0:T(128)} %starts_hbm.1, f32[20,512]{1,0:T(8,128)} %step_hbm.1, f32[1,20]{1,0:T(1,128)} %bitcast.3, f32[1,20]{1,0:T(1,128)} %bitcast.4, f32[1,20]{1,0:T(1,128)} %bitcast.5, f32[1280]{0:T(1024)} %gain_hbm.1, bf16[512,128]{1,0:T(8,128)(2,1)} %in_hbm.1, bf16[512,128]{1,0:T(8,128)(2,1)} %out_hbm.1, ...), custom_call_target="tpu_custom_call" | custom-call | tf_op jit(solution)/shard_map/pallas_call | solution.py:723
  31.8 0.8 %copy.13 = bf16[128,2560]{1,0:T(8,128)(2,1)} copy(bf16[128,2560]{1,0:T(8,128)(2,1)S(1)} %shard_map.109) | data formatting | bytes 1310720

commit v6 on v5

--- a/solution.py
+++ b/solution.py
@@ -494,12 +494,6 @@
         finish(k, pl.ds(0, rows))
         return 0
 
-    lax.fori_loop(jnp.where(carries, chunks - LAG, 0), chunks - 1, finish_step, 0)
-    for j in range(READY):
-        held[j] = product(half_rows(1 - side), early_depth, j)
-    take(chunks - 1)
-    finish(chunks - 1, half_rows(1 - side))
-
     def near_copy(stage, j, sem):
         at = stage * pieces + j
         return remote(outbox.at[at], near_in.at[at], sent, sem, s, near)
@@ -546,6 +540,13 @@
         outbox[at] = held[at, core_rows(1 - core), :].astype(BF16)
         near_copy(stage, j, near_recv.at[j] if stage == 0 else near_last).start()
 
+    def far_rows(which):
+        return pl.ds(pl.multiple_of((1 - side) * half + which * share, share), share)
+
+    def add_late(which):
+        part = product(far_rows(which), late_depth, 0)
+        held[0, core_rows(which), :] = held[0, core_rows(which), :] + part
+
     def project(stage, which, j):
         at = stage * pieces + j
         held[at] = product(half_rows(which), pl.ds(0, channels), j)
@@ -583,8 +584,18 @@
         for i in range(len(peers)):
             square_copy(i).start()
 
+    lax.fori_loop(jnp.where(carries, chunks - LAG, 0), chunks - 1, finish_step, 0)
+    for j in range(READY):
+        held[j] = product(half_rows(1 - side), early_depth, j)
+    take(chunks - 1)
+    finish(chunks - 1, far_rows(1 - core))
+    add_late(1 - core)
+    exchange(0, 0)
+    finish(chunks - 1, far_rows(core))
+    add_late(core)
+
     def far_step(j, _):
-        @pl.when(j < READY)
+        @pl.when((j > 0) & (j < READY))
         def _():
             held[j] = held[j] + product(half_rows(1 - side), late_depth, j)
 
@@ -592,7 +603,7 @@
         def _():
             project(0, 1 - side, j)
 
-        @pl.when((j < pieces - 1) | ((j == pieces - 1) & (core == 0)))
+        @pl.when(((j > 0) & (j < pieces - 1)) | ((j == pieces - 1) & (core == 0)))
         def _():
             exchange(0, j)
 

time: 32.8 us -> 32.7 us (level)
  no operation moved by 1% of the time
where the time goes in v6:
time: 32.7 us; the launch traced here: 32.5 us
  Pallas kernels  31.7 us (97%)
  local copies, waits for them, and re-layouts  0.84 us (3%)
    pallas_call x1, Pallas kernels, local(): pl.pallas_call(functools.partial(kernel, n_seq, n_head, heads, chunks, pi...  31.7 us
    unnamed x1, local copies, waits for them, and re-layouts  0.84 us

profile of v6, /device:TPU:17, one launch (start us, length us, event | category | flops | bytes accessed | tf_op | source)
XLA Modules:
  0.0 32.5 jit_solution(4536019411579347449)
XLA Ops:
  0.0 31.7 %shard_map.109 = bf16[128,2560]{1,0:T(8,128)(2,1)S(1)} custom-call(s32[16]{0:T(128)} %starts_hbm.1, f32[20,512]{1,0:T(8,128)} %step_hbm.1, f32[1,20]{1,0:T(1,128)} %bitcast.3, f32[1,20]{1,0:T(1,128)} %bitcast.4, f32[1,20]{1,0:T(1,128)} %bitcast.5, f32[1280]{0:T(1024)} %gain_hbm.1, bf16[512,128]{1,0:T(8,128)(2,1)} %in_hbm.1, bf16[512,128]{1,0:T(8,128)(2,1)} %out_hbm.1, ...), custom_call_target="tpu_custom_call" | custom-call | tf_op jit(solution)/shard_map/pallas_call | solution.py:734
  31.7 0.8 %copy.13 = bf16[128,2560]{1,0:T(8,128)(2,1)} copy(bf16[128,2560]{1,0:T(8,128)(2,1)S(1)} %shard_map.109) | data formatting | bytes 1310720

commit v7 on v6

--- a/solution.py
+++ b/solution.py
@@ -16,8 +16,8 @@
 FAR_LAG = 2
 READY = 2
 SOON = 1
-LAG = 3
-LENT = ((2, 2), (1, 0))
+LAG = 4
+LENT = ((2, 2), (0, 1))
 SLOTS = max(max(counts) for counts in LENT)
 
 

time: 32.7 us -> 32.5 us (level)
  no operation moved by 1% of the time
where the time goes in v7:
time: 32.5 us; the launch traced here: 32.4 us
  Pallas kernels  31.5 us (97%)
  local copies, waits for them, and re-layouts  0.84 us (3%)
    pallas_call x1, Pallas kernels, local(): pl.pallas_call(functools.partial(kernel, n_seq, n_head, heads, chunks, pi...  31.5 us
    unnamed x1, local copies, waits for them, and re-layouts  0.84 us

profile of v7, /device:TPU:17, one launch (start us, length us, event | category | flops | bytes accessed | tf_op | source)
XLA Modules:
  0.0 32.4 jit_solution(4638626096731658664)
XLA Ops:
  0.0 31.5 %shard_map.109 = bf16[128,2560]{1,0:T(8,128)(2,1)S(1)} custom-call(s32[16]{0:T(128)} %starts_hbm.1, f32[20,512]{1,0:T(8,128)} %step_hbm.1, f32[1,20]{1,0:T(1,128)} %bitcast.3, f32[1,20]{1,0:T(1,128)} %bitcast.4, f32[1,20]{1,0:T(1,128)} %bitcast.5, f32[1280]{0:T(1024)} %gain_hbm.1, bf16[512,128]{1,0:T(8,128)(2,1)} %in_hbm.1, bf16[512,128]{1,0:T(8,128)(2,1)} %out_hbm.1, ...), custom_call_target="tpu_custom_call" | custom-call | tf_op jit(solution)/shard_map/pallas_call | solution.py:734
  31.5 0.8 %copy.13 = bf16[128,2560]{1,0:T(8,128)(2,1)} copy(bf16[128,2560]{1,0:T(8,128)(2,1)S(1)} %shard_map.109) | data formatting | bytes 1310720
